TPU v7x, 512 devices: a 8x2x16 block of a 8x8x16 slice. The times are simulated.
512 devices in a mesh: groups: 2 (over y), seq: 16 (over z), exp: 8 (over x), tp: 2 (over core).
Axes of the slice: x: 8, y: 2, z: 16, core: 2. Of those that a mesh axis runs over, the one named last changes fastest.
The devices are a block of a 8x8x16 slice.
Arguments:
- attn_query: bfloat16 [8192, 1152], P(('groups', 'seq'), ('exp', 'tp')), parts along dimension 0, may hold values from -6 to 6
- fresh_keys: bfloat16 [8192, 1152], P(('groups', 'seq'), ('exp', 'tp')), parts along dimension 0, may hold values from -6 to 6
- fresh_values: bfloat16 [8192, 1152], P(('groups', 'seq'), ('exp', 'tp')), parts along dimension 0, may hold values from -6 to 6
- stale_keys: bfloat16 [8192, 1152], P(('groups', 'seq'), ('exp', 'tp')), parts along dimension 0, may hold values from -6 to 6
- stale_values: bfloat16 [8192, 1152], P(('groups', 'seq'), ('exp', 'tp')), parts along dimension 0, may hold values from -6 to 6
- block_flags: int32 [64], P(('groups', 'seq')), parts along dimension 0, may hold values 0 or 1
- moe_tokens: bfloat16 [65536, 1152], P(('groups', 'seq', 'exp', 'tp')), parts along dimension 0, may hold values from -6 to 6
- expert_ids: int32 [65536, 2], P(('groups', 'seq', 'exp', 'tp')), parts along dimension 0, may hold values from 0 to 15, all different within a row; in each aligned block of 128 rows (0 to 127, 128 to 255, ...) at most 20 rows name the same one
- gate_weights: float32 [65536, 2], P(('groups', 'seq', 'exp', 'tp')), parts along dimension 0, may hold values from 0.25 to 1
- up_weight: bfloat16 [16, 1152, 4608], P('seq', None, ('exp', 'tp')), may hold values from -0.1875 to 0.1875
- up_bias: float32 [16, 4608], P('seq', ('exp', 'tp')), may hold values from -3 to 3
- down_weight: bfloat16 [16, 4608, 1152], P('seq', ('exp', 'tp')), may hold values from -0.09375 to 0.09375
- down_bias: float32 [16, 1152], P('seq'), may hold values from -2 to 2
Outputs:
- attn_out: bfloat16 [8192, 1152], P(('groups', 'seq'), ('exp', 'tp')), parts along dimension 0
- moe_out: bfloat16 [65536, 1152], P(('groups', 'seq', 'exp', 'tp')), parts along dimension 0
There are 2 independent parts, one for each index of `groups`. A program takes and returns all parts, laid end to end along the dimension named above; an argument that names none is the same for every part. Nothing has to cross between parts.
Inputs may be any that keep to these rules, and one draw needn't show every extreme that they name: `expert_ids`: the 2 ids of a token differ. In the rows of one device no expert is named more than 20 times, and in every draw some expert is named exactly 20 times in some device's rows.
All inputs are finite; a program needn't handle non-finite values. No bound on the sum of `block_flags` on one device may be relied on, other than what follows from the above.
Results may differ from a plain program's by a relative error of at most 0.014.
Values may be sent and summed in bfloat16 or wider, within the bound.
No kernel may reach another device: no remote copies, remote signals or barrier semaphores. Data moves between devices by JAX's collectives and lax.ppermute only.
A program may use at most 64 MiB of HBM per device.

v0:
```python
import functools
import math

import jax
import jax.numpy as jnp
from jax import lax
from jax.experimental import pallas as pl
from jax.experimental.pallas import tpu as pltpu
from jax.sharding import PartitionSpec as P


HD = 72
ROWS = 8
LANES = 128
BF = jnp.bfloat16
F32 = jnp.float32


def shifted(value, axis, step):
    size = lax.axis_size(axis)
    return lax.ppermute(value, axis, [(i, (i + step) % size) for i in range(size)])


def after(value, *others):
    return lax.optimization_barrier((value, *others))[0]


def to_each(value, axis, groups):
    copies = jnp.broadcast_to(value[None], (len(groups[0]), *value.shape))
    moved = lax.all_to_all(copies, axis, 0, 0, axis_index_groups=groups, tiled=True)
    return moved.reshape(len(groups[0]) * value.shape[0], *value.shape[1:])


def dot(a, b, over_a=1, over_b=0):
    return lax.dot_general(a, b, (((over_a,), (over_b,)), ((), ())), preferred_element_type=F32)


def call(body, outs, flops, aliases=None, smem=(), scratch=()):
    def run(*args):
        specs = [
            pl.BlockSpec(memory_space=pltpu.SMEM if i in smem else pltpu.VMEM)
            for i in range(len(args))
        ]
        many = isinstance(outs, (list, tuple))
        shapes = list(outs) if many else [outs]
        size = sum(math.prod(s.shape) * s.dtype.itemsize for s in (*args, *shapes))
        out_specs = [pl.BlockSpec(memory_space=pltpu.VMEM) for _ in shapes]
        return pl.pallas_call(
            body,
            out_shape=shapes if many else shapes[0],
            in_specs=specs,
            out_specs=out_specs if many else out_specs[0],
            input_output_aliases=aliases or {},
            scratch_shapes=list(scratch),
            compiler_params=pltpu.CompilerParams(vmem_limit_bytes=32 << 20),
            cost_estimate=pl.CostEstimate(flops=flops, bytes_accessed=size, transcendentals=0),
        )(*args)

    return run


def shape(dims, dtype):
    return jax.ShapeDtypeStruct(dims, dtype)


def pack_weights_body(up, bias, down, out):
    hidden, width = up.shape
    out[:hidden, :] = up[...]
    row = bias[...]
    high = row.astype(BF)
    low = (row - high.astype(F32)).astype(BF)
    slab = jnp.concatenate(
        [high.astype(F32), low.astype(F32), jnp.zeros((ROWS - 2, hidden), F32)], axis=0
    )
    slab = jnp.concatenate([slab, jnp.zeros((ROWS, width - hidden), F32)], axis=1)
    out[hidden : hidden + ROWS, :] = slab.astype(BF)
    out[hidden + ROWS :, :] = down[...]


def dispatch_body(number, capacity, ids, gates, tokens, buffer, high, low):
    count = ids.shape[1]
    group = number * ROWS
    name = lax.broadcasted_iota(jnp.int32, (number, count), 0)
    first = (ids[0:1, :] == name).astype(F32)
    second = (ids[1:2, :] == name).astype(F32)
    above = lax.broadcasted_iota(jnp.int32, (count, count), 1)
    earlier = (lax.broadcasted_iota(jnp.int32, (count, count), 0) < above).astype(BF)
    before = dot((first + second).astype(BF), earlier)
    place0 = jnp.sum(before * first, axis=0, keepdims=True).astype(jnp.int32)
    place1 = jnp.sum((before + first) * second, axis=0, keepdims=True).astype(jnp.int32)
    slot0 = ids[0:1, :] * capacity + place0
    slot1 = ids[1:2, :] * capacity + place1
    line = lax.broadcasted_iota(jnp.int32, (4 * group, count), 0)
    part = line // group
    expert = (line % group) // ROWS
    row = line % ROWS
    place = jnp.where(part < 2, part * ROWS + row, 2 * ROWS + row % (ROWS // 2))
    lower = jnp.where(row < ROWS // 2, 2, 3)
    code = jnp.where((part < 2) | (part == lower), expert * capacity + place, -1)
    match0 = jnp.where(slot0 == code, 1.0, 0.0)
    match1 = jnp.where(slot1 == code, 1.0, 0.0)
    table = match0 + match1
    weight = match0 * gates[0:1, :] + match1 * gates[1:2, :]
    top = weight.astype(BF)
    high[...] = top
    low[...] = (weight - top.astype(F32)).astype(BF)
    ends = jnp.concatenate(
        [table[: 2 * group], table[2 * group : 3 * group] + table[3 * group :]], axis=0
    ).astype(BF)
    rows = dot(ends, tokens[...]).astype(BF)
    pack(buffer, rows[:group], rows[group : 2 * group], rows[2 * group :])


def split_of(width):
    return (width // LANES + 1) // 2 * LANES


def pack(buffer, first, second, ends):
    width = first.shape[1]
    cut = split_of(width)
    buffer[:, :width] = first
    buffer[:, width : 2 * width] = second
    row = lax.broadcasted_iota(jnp.int32, (ends.shape[0], 1), 0) % ROWS
    lower = ends[:, :cut].astype(F32)
    upper = jnp.concatenate(
        [ends[:, cut:].astype(F32), jnp.zeros((ends.shape[0], 2 * cut - width), F32)], axis=1
    )
    buffer[:, 2 * width :] = jnp.where(row < ROWS // 2, lower, upper).astype(BF)


def halves(group, half):
    out_row = lax.broadcasted_iota(jnp.int32, (group // 2, group), 0)
    in_row = lax.broadcasted_iota(jnp.int32, (group // 2, group), 1)
    short = ROWS // 2
    return (in_row == out_row // short * ROWS + out_row % short + half * short).astype(BF)


def unpack_body(own, other, rows):
    group = own.shape[0]
    width = rows.shape[1]
    cut = split_of(width)
    base = rows.shape[0] // 2
    for k, ref in enumerate((own, other)):
        at = k * base
        rows[at : at + group, :] = ref[:, :width]
        rows[at + group : at + 2 * group, :] = ref[:, width : 2 * width]
        ends = ref[:, 2 * width :]
        rows[at + 2 * group : at + base, :cut] = dot(halves(group, 0), ends).astype(BF)
        rows[at + 2 * group : at + base, cut:] = dot(
            halves(group, 1), ends[:, : width - cut]
        ).astype(BF)


def contribution(rows, up, bias, down):
    raised = dot(rows, up, 1, 1) + bias
    return dot(jax.nn.gelu(raised).astype(BF), down)


def bias_of(slab):
    return slab[0:1, :].astype(F32) + slab[1:2, :].astype(F32)


def steps_body(pieces, rows, *refs):
    *ins, total, ups, downs = refs
    hidden = (ins[0].shape[0] - ROWS) // 2
    slabs = []
    for k, piece in enumerate(ins[:pieces]):
        at = k * hidden
        ups[at : at + hidden, :] = piece[:hidden, :]
        downs[at : at + hidden, :] = piece[hidden + ROWS :, :]
        slabs.append(bias_of(piece[hidden : hidden + ROWS, :hidden]))
    bias = jnp.concatenate(slabs, axis=1)
    count = rows.shape[0]
    size = count // 4
    for at in range(0, count, size):
        part = contribution(rows[at : at + size, :], ups[...], bias, downs[...])
        if len(ins) > pieces:
            part += ins[pieces][at : at + size, :]
        total[at : at + size, :] = part


def last_body(rows, upper, lower, old, own, other):
    hidden = lower.shape[0]
    total = old[...] + contribution(
        rows[...], upper[:hidden, :], bias_of(upper[hidden:, :hidden]), lower[...]
    )
    half = own.shape[0]
    own[...] = total[:half]
    other[...] = total[half:].astype(BF)


def reduce_body(own, other, bias, buffer):
    group = buffer.shape[0]
    total = (own[...] + other[...].astype(F32) + bias[...]).astype(BF)
    tail = total[2 * group :]
    ends = dot(halves(group, 0), tail, 0, 0) + dot(halves(group, 1), tail, 0, 0)
    pack(buffer, total[:group], total[group : 2 * group], ends.astype(BF))


def combine_body(high, low, buffer, out):
    group = buffer.shape[0]
    width = out.shape[1]
    cut = split_of(width)
    total = None
    for gates in (high, low):
        part = dot(gates[:group, :], buffer[:, :width], 0, 0)
        part += dot(gates[group : 2 * group, :], buffer[:, width : 2 * width], 0, 0)
        lower = dot(gates[2 * group : 3 * group, :], buffer[:, 2 * width :], 0, 0)
        upper = dot(gates[3 * group :, :], buffer[:, 2 * width : 3 * width - cut], 0, 0)
        part += jnp.concatenate([lower, upper], axis=1)
        total = part if total is None else total + part
    out[...] = total.astype(BF)


def select_body(flags, new_keys, new_values, old_keys, old_values, out):
    width, length = new_keys.shape
    block = length // flags.shape[0]
    place = lax.broadcasted_iota(jnp.int32, (width, length), 1) // block
    fresh = jnp.zeros((width, length), jnp.int32)
    for k in range(flags.shape[0]):
        fresh = jnp.where(place == k, flags[k], fresh)
    for k, (new, old) in enumerate(((new_keys, old_keys), (new_values, old_values))):
        chosen = jnp.where(fresh == 1, new[...].astype(F32), old[...].astype(F32))
        out[k * width : (k + 1) * width, :] = chosen.astype(BF)


def attend_body(query, gathered, out):
    width = query.shape[0]
    sources = gathered.shape[0] // (2 * width)
    for head in range(width // HD):
        at = head * HD
        scale = 1.0 / math.sqrt(HD)
        keys = [gathered[2 * width * k + at : 2 * width * k + at + HD, :] for k in range(sources)]
        values = [
            gathered[2 * width * k + width + at : 2 * width * k + width + at + HD, :]
            for k in range(sources)
        ]
        scores = [dot(k, query[at : at + HD, :], 0, 0) * scale for k in keys]
        highest = functools.reduce(
            jnp.maximum, [jnp.max(s, axis=0, keepdims=True) for s in scores]
        )
        totals = mixed = 0.0
        for s, v in zip(scores, values):
            probs = jnp.exp(s - highest)
            totals += jnp.sum(probs, axis=0, keepdims=True)
            mixed += dot(v, probs.astype(BF))
        out[at : at + HD, :] = (mixed / totals).astype(BF)


def local(
    attn_query,
    fresh_keys,
    fresh_values,
    stale_keys,
    stale_values,
    block_flags,
    moe_tokens,
    expert_ids,
    gate_weights,
    up_weight,
    up_bias,
    down_weight,
    down_bias,
):
    width, hidden = up_weight.shape[1:]
    length = attn_query.shape[0]
    tokens_here = moe_tokens.shape[0]
    number = lax.axis_size("seq") * up_weight.shape[0]
    capacity = 5 * tokens_here // (2 * number)
    slots = number * capacity
    group = number * ROWS
    packed = (group, 2 * width + split_of(width))
    ring = lax.axis_size("exp")
    work = 8 * slots * width * hidden

    own_piece = call(
        pack_weights_body, shape((2 * hidden + ROWS, width), BF), 1 << 28
    )(up_weight[0].T, up_bias, down_weight[0])
    passed = [(shifted(own_piece, "exp", 1), shifted(own_piece, "exp", -1))]
    for _ in range(2, ring // 2):
        right, left = passed[-1]
        passed.append((shifted(right, "exp", 1), shifted(left, "exp", -1)))

    own_kv = call(select_body, shape((2 * attn_query.shape[1], length), BF), 1 << 24, smem=(0,))(
        block_flags, fresh_keys.T, fresh_values.T, stale_keys.T, stale_values.T
    )
    size = lax.axis_size("seq")
    near = math.gcd(size, 4)
    far_kv = jnp.concatenate(
        [own_kv] + [shifted(own_kv, "seq", near * k) for k in range(1, size // near)], axis=0
    )

    buffer, high, low = call(
        functools.partial(dispatch_body, number, capacity),
        [shape(packed, BF), shape((4 * group, tokens_here), BF), shape((4 * group, tokens_here), BF)],
        1 << 27,
    )(expert_ids.T, gate_weights.T, moe_tokens)

    def exchanged(value):
        parts = value.reshape(number, ROWS, packed[1])
        moved = lax.all_to_all(parts, "seq", split_axis=0, concat_axis=0, tiled=True)
        return moved.reshape(packed)

    received = exchanged(buffer)
    received = after(received, passed[1])

    runs = [[near * a + b for b in range(near)] for a in range(size // near)]
    gathered = to_each(after(far_kv, received), "seq", runs)

    rows = call(unpack_body, shape((2 * slots, width), BF), 1 << 28)(
        received, shifted(received, "tp", 1)
    )

    def steps(pieces, old=None):
        extra = [] if old is None else [old]
        both = pltpu.VMEM((len(pieces) * hidden, width), BF)
        return call(
            functools.partial(steps_body, len(pieces)),
            shape((2 * slots, width), F32),
            len(pieces) * work,
            aliases={len(pieces) + 1: 0} if extra else None,
            scratch=(both, both),
        )(rows, *pieces, *extra)

    early = steps([own_piece] + [p for pair in passed[:-1] for p in pair])
    total = steps(list(passed[-1]), early)
    right, left = after(passed[-1], early, far_kv)
    upper = shifted(right[: hidden + ROWS], "exp", 1)
    lower = shifted(left[hidden + ROWS :], "exp", -1)
    own, other = call(
        last_body, [shape((slots, width), F32), shape((slots, width), BF)], work
    )(rows, upper, lower, total)
    result = call(reduce_body, shape(packed, BF), 1 << 28)(own, shifted(other, "tp", 1), down_bias)
    back = exchanged(after(result, gathered))
    attn_out = call(attend_body, shape(attn_query.shape[::-1], BF), 1 << 31)(attn_query.T, gathered)
    moe_out = call(combine_body, shape(moe_tokens.shape, BF), 1 << 29)(high, low, back)
    return (attn_out.T, moe_out)


def solution(mesh):
    in_specs = (
        P(("groups", "seq"), ("exp", "tp")),
        P(("groups", "seq"), ("exp", "tp")),
        P(("groups", "seq"), ("exp", "tp")),
        P(("groups", "seq"), ("exp", "tp")),
        P(("groups", "seq"), ("exp", "tp")),
        P(("groups", "seq")),
        P(("groups", "seq", "exp", "tp"), None),
        P(("groups", "seq", "exp", "tp"), None),
        P(("groups", "seq", "exp", "tp"), None),
        P("seq", None, ("exp", "tp")),
        P("seq", ("exp", "tp")),
        P("seq", ("exp", "tp"), None),
        P("seq", None),
    )
    out_specs = (P(("groups", "seq"), ("exp", "tp")), P(("groups", "seq", "exp", "tp"), None))

    return jax.shard_map(local, mesh=mesh, in_specs=in_specs, out_specs=out_specs, check_vma=False)
```

profile of v0, /device:TPU:68, one launch (start us, length us, event | category | flops | bytes accessed | tf_op | source)
XLA Modules:
  0.0 245.3 jit_solution(16046987283573162909)
XLA Ops:
  0.7 1.1 copy-done.15
  1.7 0.7 copy-done.17
  2.4 0.7 copy-done.18
  3.1 1.5 shard_map.141
  4.6 0.7 copy-done.19
  5.2 0.6 copy-done.21
  5.8 43.7 %all-to-all-start = ((bf16[16,8,2944]{2,1,0:T(8,128)(2,1)}), bf16[16,8,2944]{2,1,0:T(8,128)(2,1)S(1)}, u32[]{:S(2)}, u32[]{:S(2)}) async-start(bf16[16,8,2944]{2,1,0:T(8,128)(2,1)} %bitcast.7), calls=%async_computation | async-start | bytes 1507328 | tf_op jit(solution)/shard_map/all_to_all | solution.py:301
  49.5 0.0 copy-start.2
  49.6 0.1 shard_map.142.refs_0_
  49.7 3.6 %collective-permute-start.3 = (bf16[584,1152]{1,0:T(8,128)(2,1)S(1)}, bf16[584,1152]{1,0:T(8,128)(2,1)S(1)}, u32[]{:S(2)}, u32[]{:S(2)}) collective-permute-start(bf16[584,1152]{1,0:T(8,128)(2,1)S(1)} %shard_map.142.refs_0_), channel_id=1, source_target_pairs={{0,2},{2,4},{4,6},{6,8},{8,10},{10,12},{12,14},{14,0},{1,3},{3,5},... | collective-permute-start | bytes 4036616 | tf_op jit(solution)/shard_map/ppermute | solution.py:21
  53.3 2.3 collective-permute-start.5
  55.7 27.1 %collective-permute-done.3.refs_1_ = bf16[584,1152]{1,0:T(8,128)(2,1)S(1)} collective-permute-done((bf16[584,1152]{1,0:T(8,128)(2,1)S(1)}, bf16[584,1152]{1,0:T(8,128)(2,1)S(1)}, u32[]{:S(2)}, u32[]{:S(2)}) %collective-permute-start.3) | collective-permute-done | bytes 1345568 | tf_op jit(solution)/shard_map/ppermute | solution.py:21
  82.7 3.9 %collective-permute-start.4 = (bf16[584,1152]{1,0:T(8,128)(2,1)S(1)}, bf16[584,1152]{1,0:T(8,128)(2,1)S(1)}, u32[]{:S(2)}, u32[]{:S(2)}) collective-permute-start(bf16[584,1152]{1,0:T(8,128)(2,1)S(1)} %collective-permute-done.3.refs_1_), channel_id=1, source_target_pairs={{0,2},{2,4},{4,6},{6,8},{8,10},{10,12},{12,14},{14,0},{1,3},{3,5},... | collective-permute-start | bytes 4036616 | tf_op jit(solution)/shard_map/ppermute | solution.py:21
  86.6 1.1 copy-done.9
  87.7 2.0 collective-permute-start.6
  89.7 1.1 copy-done.11
  90.8 0.6 shard_map.140
  91.4 7.3 %collective-permute-start = (bf16[144,256]{1,0:T(8,128)(2,1)S(1)}, bf16[144,256]{1,0:T(8,128)(2,1)S(1)}, u32[]{:S(2)}, u32[]{:S(2)}) collective-permute-start(bf16[144,256]{1,0:T(8,128)(2,1)S(1)} %shard_map.140), channel_id=1, source_target_pairs={{0,64},{16,80},{32,96},{48,112},{64,128},{80,144},{96,160},{112,17... | collective-permute-start | bytes 221192 | tf_op jit(solution)/shard_map/ppermute | solution.py:21
  98.7 7.3 %collective-permute-start.1 = (bf16[144,256]{1,0:T(8,128)(2,1)S(1)}, bf16[144,256]{1,0:T(8,128)(2,1)S(1)}, u32[]{:S(2)}, u32[]{:S(2)}) collective-permute-start(bf16[144,256]{1,0:T(8,128)(2,1)S(1)} %shard_map.140), channel_id=1, source_target_pairs={{0,128},{16,144},{32,160},{48,176},{64,192},{80,208},{96,224},{112... | collective-permute-start | bytes 221192 | tf_op jit(solution)/shard_map/ppermute | solution.py:21
  106.0 7.3 %collective-permute-start.2 = (bf16[144,256]{1,0:T(8,128)(2,1)S(1)}, bf16[144,256]{1,0:T(8,128)(2,1)S(1)}, u32[]{:S(2)}, u32[]{:S(2)}) collective-permute-start(bf16[144,256]{1,0:T(8,128)(2,1)S(1)} %shard_map.140), channel_id=1, source_target_pairs={{0,192},{16,208},{32,224},{48,240},{64,0},{80,16},{96,32},{112,48}... | collective-permute-start | bytes 221192 | tf_op jit(solution)/shard_map/ppermute | solution.py:21
  113.3 0.7 collective-permute-done.1
  114.1 6.6 %collective-permute-done.2 = bf16[144,256]{1,0:T(8,128)(2,1)S(1)} collective-permute-done((bf16[144,256]{1,0:T(8,128)(2,1)S(1)}, bf16[144,256]{1,0:T(8,128)(2,1)S(1)}, u32[]{:S(2)}, u32[]{:S(2)}) %collective-permute-start.2) | collective-permute-done | bytes 73760 | tf_op jit(solution)/shard_map/ppermute | solution.py:21
  120.7 1.1 copy-done.13
  121.9 1.1 broadcast_in_dim.2
  122.9 4.0 %all-to-all-start.1 = ((bf16[4,576,256]{2,1,0:T(8,128)(2,1)}), bf16[4,576,256]{2,1,0:T(8,128)(2,1)S(1)}, u32[]{:S(2)}, u32[]{:S(2)}) async-start(bf16[4,576,256]{2,1,0:T(8,128)(2,1)} %broadcast_in_dim.2), calls=%async_computation.1 | async-start | bytes 2359296 | tf_op jit(solution)/shard_map/all_to_all | solution.py:30
  126.9 5.5 %collective-permute-start.8 = (bf16[584,1152]{1,0:T(8,128)(2,1)}, bf16[584,1152]{1,0:T(8,128)(2,1)S(1)}, u32[]{:S(2)}, u32[]{:S(2)}) collective-permute-start(bf16[584,1152]{1,0:T(8,128)(2,1)} %copy-done.13), channel_id=1, source_target_pairs={{0,2},{2,4},{4,6},{6,8},{8,10},{10,12},{12,14},{14,0},{1,3},{3,5},... | collective-permute-start | bytes 4036616 | tf_op jit(solution)/shard_map/ppermute | solution.py:21
  132.5 2.0 collective-permute-start.9
  134.5 2.0 collective-permute-start.7
  136.4 2.2 collective-permute-done.7.other
  138.6 0.4 shard_map.144.rows
  139.0 1.3 copy-done.14
  140.3 8.4 %shard_map.145.refs_2_ = f32[640,1152]{1,0:T(8,128)S(1)} custom-call(bf16[640,1152]{1,0:T(8,128)(2,1)S(1)} %shard_map.144.rows, bf16[584,1152]{1,0:T(8,128)(2,1)S(1)} %shard_map.142.refs_0_, bf16[584,1152]{1,0:T(8,128)(2,1)S(1)} %copy-done.10, bf16[584,1152]{1,0:T(8,128)(2,1)S(1)} %copy-done.12, bf16[584,1152]{1,0:T(8,128)(2,1)S(1)} %copy-done.14, ...), custom_call_target="tpu_custom_call" | custom-call | flops 4246732800 | bytes 11151360 | tf_op jit(solution)/shard_map/pallas_call | solution.py:48
  148.7 12.8 %collective-permute-done.8.refs_0_ = bf16[584,1152]{1,0:T(8,128)(2,1)S(1)} collective-permute-done((bf16[584,1152]{1,0:T(8,128)(2,1)}, bf16[584,1152]{1,0:T(8,128)(2,1)S(1)}, u32[]{:S(2)}, u32[]{:S(2)}) %collective-permute-start.8) | collective-permute-done | bytes 1345568 | tf_op jit(solution)/shard_map/ppermute | solution.py:21
  161.5 5.1 %collective-permute-done.9.refs_1_ = bf16[584,1152]{1,0:T(8,128)(2,1)S(1)} collective-permute-done((bf16[584,1152]{1,0:T(8,128)(2,1)}, bf16[584,1152]{1,0:T(8,128)(2,1)S(1)}, u32[]{:S(2)}, u32[]{:S(2)}) %collective-permute-start.9) | collective-permute-done | bytes 1345568 | tf_op jit(solution)/shard_map/ppermute | solution.py:21
  166.6 0.1 slice.6
  166.7 4.9 %collective-permute-start.10 = (bf16[296,1152]{1,0:T(8,128)(2,1)S(1)}, bf16[296,1152]{1,0:T(8,128)(2,1)S(1)}, u32[]{:S(2)}, u32[]{:S(2)}) collective-permute-start(bf16[296,1152]{1,0:T(8,128)(2,1)S(1)} %slice.6), channel_id=1, source_target_pairs={{0,2},{2,4},{4,6},{6,8},{8,10},{10,12},{12,14},{14,0},{1,3},{3,5},... | collective-permute-start | bytes 2045960 | tf_op jit(solution)/shard_map/ppermute | solution.py:21
  171.6 0.1 slice.7
  171.6 2.1 collective-permute-start.11
  173.8 4.1 %shard_map.146.old = f32[640,1152]{1,0:T(8,128)S(1)} custom-call(bf16[640,1152]{1,0:T(8,128)(2,1)S(1)} %shard_map.144.rows, bf16[584,1152]{1,0:T(8,128)(2,1)S(1)} %collective-permute-done.8.refs_0_, bf16[584,1152]{1,0:T(8,128)(2,1)S(1)} %collective-permute-done.9.refs_1_, f32[640,1152]{1,0:T(8,128)S(1)} %shard_map.145.refs_2_), custom_call_target="tpu_custom_call", output_to_operand_aliasing={{}: (3, {})} | custom-call | flops 1698693120 | bytes 10063872 | tf_op jit(solution)/shard_map/pallas_call | solution.py:48
  177.9 10.9 %collective-permute-done.11.lower = bf16[288,1152]{1,0:T(8,128)(2,1)S(1)} collective-permute-done((bf16[288,1152]{1,0:T(8,128)(2,1)S(1)}, bf16[288,1152]{1,0:T(8,128)(2,1)S(1)}, u32[]{:S(2)}, u32[]{:S(2)}) %collective-permute-start.11) | collective-permute-done | bytes 663584 | tf_op jit(solution)/shard_map/ppermute | solution.py:21
  188.8 2.0 shard_map.147
  190.8 2.0 collective-permute-start.12
  192.8 2.2 collective-permute-done.12.other
  194.9 1.5 shard_map.148
  196.5 9.4 %all-to-all-start.2 = ((bf16[16,8,2944]{2,1,0:T(8,128)(2,1)}), bf16[16,8,2944]{2,1,0:T(8,128)(2,1)S(1)}, u32[]{:S(2)}, u32[]{:S(2)}) async-start(bf16[16,8,2944]{2,1,0:T(8,128)(2,1)} %bitcast.14), calls=%async_computation.2 | async-start | bytes 1507328 | tf_op jit(solution)/shard_map/all_to_all | solution.py:301
  205.9 2.7 %shard_map.143 = bf16[72,256]{1,0:T(8,128)(2,1)} custom-call(bf16[72,256]{1,0:T(8,128)(2,1)S(1)} %bitcast.27, bf16[2304,256]{1,0:T(8,128)(2,1)S(1)} %bitcast.19), custom_call_target="tpu_custom_call" | custom-call | flops 2147483648 | bytes 1253376 | tf_op jit(solution)/shard_map/pallas_call | solution.py:48
  208.7 35.2 %all-to-all-done.2 = bf16[16,8,2944]{2,1,0:T(8,128)(2,1)S(1)} async-done(((bf16[16,8,2944]{2,1,0:T(8,128)(2,1)}), bf16[16,8,2944]{2,1,0:T(8,128)(2,1)S(1)}, u32[]{:S(2)}, u32[]{:S(2)}) %all-to-all-start.2) | async-done | bytes 753696 | tf_op jit(solution)/shard_map/all_to_all | solution.py:301
  243.9 1.4 shard_map.149
  (44 shorter events, 0.1 us)
Async XLA Ops:
  0.6 49.0 %copy-start = (bf16[1,1152,288]{1,2,0:T(8,128)(2,1)S(1)}, bf16[1,1152,288]{1,2,0:T(8,128)(2,1)}, u32[]{:S(2)}) copy-start(bf16[1,1152,288]{1,2,0:T(8,128)(2,1)} %param.22) | copy-start | bytes 1990660
  0.6 49.0 %copy-start.1 = (bf16[1,288,1152]{2,1,0:T(8,128)(2,1)S(1)}, bf16[1,288,1152]{2,1,0:T(8,128)(2,1)}, u32[]{:S(2)}) copy-start(bf16[1,288,1152]{2,1,0:T(8,128)(2,1)} %param.24) | copy-start | bytes 1990660
  0.7 49.0 %copy-start.7 = (f32[1,288]{1,0:T(1,128)S(1)}, f32[1,288]{1,0:T(1,128)}, u32[]{:S(2)}) copy-start(f32[1,288]{1,0:T(1,128)} %bias.2) | copy-start | bytes 3460
  0.7 1.1 copy-start.15
  1.7 0.7 copy-start.17
  2.4 0.7 copy-start.18
  4.5 0.7 copy-start.19
  5.2 0.6 copy-start.21
  5.8 116.0 %all-to-all-start = ((bf16[16,8,2944]{2,1,0:T(8,128)(2,1)}), bf16[16,8,2944]{2,1,0:T(8,128)(2,1)S(1)}, u32[]{:S(2)}, u32[]{:S(2)}) async-start(bf16[16,8,2944]{2,1,0:T(8,128)(2,1)} %bitcast.7), calls=%async_computation | async-start | bytes 1507328 | tf_op jit(solution)/shard_map/all_to_all | solution.py:301
  49.5 41.3 %copy-start.2 = (bf16[256,72]{0,1:T(8,128)(2,1)S(1)}, bf16[256,72]{0,1:T(8,128)(2,1)}, u32[]{:S(2)}) copy-start(bf16[256,72]{0,1:T(8,128)(2,1)} %param.14) | copy-start | bytes 110596
  49.5 41.3 %copy-start.3 = (bf16[256,72]{0,1:T(8,128)(2,1)S(1)}, bf16[256,72]{0,1:T(8,128)(2,1)}, u32[]{:S(2)}) copy-start(bf16[256,72]{0,1:T(8,128)(2,1)} %param.15) | copy-start | bytes 110596
  49.6 41.2 %copy-start.4 = (bf16[256,72]{0,1:T(8,128)(2,1)S(1)}, bf16[256,72]{0,1:T(8,128)(2,1)}, u32[]{:S(2)}) copy-start(bf16[256,72]{0,1:T(8,128)(2,1)} %param.16) | copy-start | bytes 110596
  49.6 41.2 %copy-start.5 = (bf16[256,72]{0,1:T(8,128)(2,1)S(1)}, bf16[256,72]{0,1:T(8,128)(2,1)}, u32[]{:S(2)}) copy-start(bf16[256,72]{0,1:T(8,128)(2,1)} %param.17) | copy-start | bytes 110596
  49.6 41.2 %copy-start.8 = (s32[2]{0:T(128)S(1)}, s32[2]{0:T(128)}, u32[]{:S(2)}) copy-start(s32[2]{0:T(128)} %flags.1) | copy-start | bytes 28
  49.7 33.0 %collective-permute-start.3 = (bf16[584,1152]{1,0:T(8,128)(2,1)S(1)}, bf16[584,1152]{1,0:T(8,128)(2,1)S(1)}, u32[]{:S(2)}, u32[]{:S(2)}) collective-permute-start(bf16[584,1152]{1,0:T(8,128)(2,1)S(1)} %shard_map.142.refs_0_), channel_id=1, source_target_pairs={{0,2},{2,4},{4,6},{6,8},{8,10},{10,12},{12,14},{14,0},{1,3},{3,5},... | collective-permute-start | bytes 4036616 | tf_op jit(solution)/shard_map/ppermute | solution.py:21
  53.3 34.4 %collective-permute-start.5 = (bf16[584,1152]{1,0:T(8,128)(2,1)S(1)}, bf16[584,1152]{1,0:T(8,128)(2,1)S(1)}, u32[]{:S(2)}, u32[]{:S(2)}) collective-permute-start(bf16[584,1152]{1,0:T(8,128)(2,1)S(1)} %shard_map.142.refs_0_), channel_id=1, source_target_pairs={{0,14},{2,0},{4,2},{6,4},{8,6},{10,8},{12,10},{14,12},{1,15},{3,1}... | collective-permute-start | bytes 4036616 | tf_op jit(solution)/shard_map/ppermute | solution.py:21
  82.7 38.0 %collective-permute-start.4 = (bf16[584,1152]{1,0:T(8,128)(2,1)S(1)}, bf16[584,1152]{1,0:T(8,128)(2,1)S(1)}, u32[]{:S(2)}, u32[]{:S(2)}) collective-permute-start(bf16[584,1152]{1,0:T(8,128)(2,1)S(1)} %collective-permute-done.3.refs_1_), channel_id=1, source_target_pairs={{0,2},{2,4},{4,6},{6,8},{8,10},{10,12},{12,14},{14,0},{1,3},{3,5},... | collective-permute-start | bytes 4036616 | tf_op jit(solution)/shard_map/ppermute | solution.py:21
  86.6 1.1 copy-start.9
  87.7 34.1 %collective-permute-start.6 = (bf16[584,1152]{1,0:T(8,128)(2,1)S(1)}, bf16[584,1152]{1,0:T(8,128)(2,1)}, u32[]{:S(2)}, u32[]{:S(2)}) collective-permute-start(bf16[584,1152]{1,0:T(8,128)(2,1)S(1)} %collective-permute-done.5.refs_2_), channel_id=1, source_target_pairs={{0,14},{2,0},{4,2},{6,4},{8,6},{10,8},{12,10},{14,12},{1,15},{3,1}... | collective-permute-start | bytes 4036616 | tf_op jit(solution)/shard_map/ppermute | solution.py:21
  89.7 1.1 copy-start.11
  91.4 21.9 %collective-permute-start = (bf16[144,256]{1,0:T(8,128)(2,1)S(1)}, bf16[144,256]{1,0:T(8,128)(2,1)S(1)}, u32[]{:S(2)}, u32[]{:S(2)}) collective-permute-start(bf16[144,256]{1,0:T(8,128)(2,1)S(1)} %shard_map.140), channel_id=1, source_target_pairs={{0,64},{16,80},{32,96},{48,112},{64,128},{80,144},{96,160},{112,17... | collective-permute-start | bytes 221192 | tf_op jit(solution)/shard_map/ppermute | solution.py:21
  98.7 15.4 %collective-permute-start.1 = (bf16[144,256]{1,0:T(8,128)(2,1)S(1)}, bf16[144,256]{1,0:T(8,128)(2,1)S(1)}, u32[]{:S(2)}, u32[]{:S(2)}) collective-permute-start(bf16[144,256]{1,0:T(8,128)(2,1)S(1)} %shard_map.140), channel_id=1, source_target_pairs={{0,128},{16,144},{32,160},{48,176},{64,192},{80,208},{96,224},{112... | collective-permute-start | bytes 221192 | tf_op jit(solution)/shard_map/ppermute | solution.py:21
  106.0 14.7 %collective-permute-start.2 = (bf16[144,256]{1,0:T(8,128)(2,1)S(1)}, bf16[144,256]{1,0:T(8,128)(2,1)S(1)}, u32[]{:S(2)}, u32[]{:S(2)}) collective-permute-start(bf16[144,256]{1,0:T(8,128)(2,1)S(1)} %shard_map.140), channel_id=1, source_target_pairs={{0,192},{16,208},{32,224},{48,240},{64,0},{80,16},{96,32},{112,48}... | collective-permute-start | bytes 221192 | tf_op jit(solution)/shard_map/ppermute | solution.py:21
  120.7 1.1 copy-start.13
  122.9 73.5 %all-to-all-start.1 = ((bf16[4,576,256]{2,1,0:T(8,128)(2,1)}), bf16[4,576,256]{2,1,0:T(8,128)(2,1)S(1)}, u32[]{:S(2)}, u32[]{:S(2)}) async-start(bf16[4,576,256]{2,1,0:T(8,128)(2,1)} %broadcast_in_dim.2), calls=%async_computation.1 | async-start | bytes 2359296 | tf_op jit(solution)/shard_map/all_to_all | solution.py:30
  126.9 12.1 %copy-start.10 = (bf16[584,1152]{1,0:T(8,128)(2,1)S(1)}, bf16[584,1152]{1,0:T(8,128)(2,1)}, u32[]{:S(2)}) copy-start(bf16[584,1152]{1,0:T(8,128)(2,1)} %copy-done.9) | copy-start | bytes 4036612
  126.9 12.1 %copy-start.12 = (bf16[584,1152]{1,0:T(8,128)(2,1)S(1)}, bf16[584,1152]{1,0:T(8,128)(2,1)}, u32[]{:S(2)}) copy-start(bf16[584,1152]{1,0:T(8,128)(2,1)} %copy-done.11) | copy-start | bytes 4036612
  126.9 34.6 %collective-permute-start.8 = (bf16[584,1152]{1,0:T(8,128)(2,1)}, bf16[584,1152]{1,0:T(8,128)(2,1)S(1)}, u32[]{:S(2)}, u32[]{:S(2)}) collective-permute-start(bf16[584,1152]{1,0:T(8,128)(2,1)} %copy-done.13), channel_id=1, source_target_pairs={{0,2},{2,4},{4,6},{6,8},{8,10},{10,12},{12,14},{14,0},{1,3},{3,5},... | collective-permute-start | bytes 4036616 | tf_op jit(solution)/shard_map/ppermute | solution.py:21
  132.5 34.1 %collective-permute-start.9 = (bf16[584,1152]{1,0:T(8,128)(2,1)}, bf16[584,1152]{1,0:T(8,128)(2,1)S(1)}, u32[]{:S(2)}, u32[]{:S(2)}) collective-permute-start(bf16[584,1152]{1,0:T(8,128)(2,1)} %collective-permute-done.6.refs_4_), channel_id=1, source_target_pairs={{0,14},{2,0},{4,2},{6,4},{8,6},{10,8},{12,10},{14,12},{1,15},{3,1}... | collective-permute-start | bytes 4036616 | tf_op jit(solution)/shard_map/ppermute | solution.py:21
  134.5 4.2 %collective-permute-start.7 = (bf16[128,2944]{1,0:T(8,128)(2,1)S(1)}, bf16[128,2944]{1,0:T(8,128)(2,1)S(1)}, u32[]{:S(2)}, u32[]{:S(2)}) collective-permute-start(bf16[128,2944]{1,0:T(8,128)(2,1)S(1)} %bitcast.17), channel_id=1, source_target_pairs={{0,1},{1,0},{2,3},{3,2},{4,5},{5,4},{6,7},{7,6},{8,9},{9,8},{10,11... | collective-permute-start | bytes 2261000 | tf_op jit(solution)/shard_map/ppermute | solution.py:21
  139.0 1.3 copy-start.14
  166.7 22.1 %collective-permute-start.10 = (bf16[296,1152]{1,0:T(8,128)(2,1)S(1)}, bf16[296,1152]{1,0:T(8,128)(2,1)S(1)}, u32[]{:S(2)}, u32[]{:S(2)}) collective-permute-start(bf16[296,1152]{1,0:T(8,128)(2,1)S(1)} %slice.6), channel_id=1, source_target_pairs={{0,2},{2,4},{4,6},{6,8},{8,10},{10,12},{12,14},{14,0},{1,3},{3,5},... | collective-permute-start | bytes 2045960 | tf_op jit(solution)/shard_map/ppermute | solution.py:21
  171.6 17.1 %collective-permute-start.11 = (bf16[288,1152]{1,0:T(8,128)(2,1)S(1)}, bf16[288,1152]{1,0:T(8,128)(2,1)S(1)}, u32[]{:S(2)}, u32[]{:S(2)}) collective-permute-start(bf16[288,1152]{1,0:T(8,128)(2,1)S(1)} %slice.7), channel_id=1, source_target_pairs={{0,14},{2,0},{4,2},{6,4},{8,6},{10,8},{12,10},{14,12},{1,15},{3,1}... | collective-permute-start | bytes 1990664 | tf_op jit(solution)/shard_map/ppermute | solution.py:21
  177.9 17.0 %copy-start.6 = (f32[1,1152]{1,0:T(1,128)S(1)}, f32[1,1152]{1,0:T(1,128)}, u32[]{:S(2)}) copy-start(f32[1,1152]{1,0:T(1,128)} %bias.3) | copy-start | bytes 13828
  190.8 4.1 %collective-permute-start.12 = (bf16[320,1152]{1,0:T(8,128)(2,1)S(1)}, bf16[320,1152]{1,0:T(8,128)(2,1)S(1)}, u32[]{:S(2)}, u32[]{:S(2)}) collective-permute-start(bf16[320,1152]{1,0:T(8,128)(2,1)S(1)} %get-tuple-element.20), channel_id=1, source_target_pairs={{0,1},{1,0},{2,3},{3,2},{4,5},{5,4},{6,7},{7,6},{8,9},{9,8},{10,11... | collective-permute-start | bytes 2211848 | tf_op jit(solution)/shard_map/ppermute | solution.py:21
  196.5 9.4 %copy-start.16 = (bf16[256,72]{0,1:T(8,128)(2,1)S(1)}, bf16[256,72]{0,1:T(8,128)(2,1)}, u32[]{:S(2)}) copy-start(bf16[256,72]{0,1:T(8,128)(2,1)} %param.13) | copy-start | bytes 110596
  196.5 47.4 %all-to-all-start.2 = ((bf16[16,8,2944]{2,1,0:T(8,128)(2,1)}), bf16[16,8,2944]{2,1,0:T(8,128)(2,1)S(1)}, u32[]{:S(2)}, u32[]{:S(2)}) async-start(bf16[16,8,2944]{2,1,0:T(8,128)(2,1)} %bitcast.14), calls=%async_computation.2 | async-start | bytes 1507328 | tf_op jit(solution)/shard_map/all_to_all | solution.py:301
  205.9 38.0 %copy-start.20 = (bf16[512,128]{1,0:T(8,128)(2,1)S(1)}, bf16[512,128]{1,0:T(8,128)(2,1)}, u32[]{:S(2)}) copy-start(bf16[512,128]{1,0:T(8,128)(2,1)} %copy-done.19) | copy-start | bytes 393220
  205.9 38.0 %copy-start.22 = (bf16[512,128]{1,0:T(8,128)(2,1)S(1)}, bf16[512,128]{1,0:T(8,128)(2,1)}, u32[]{:S(2)}) copy-start(bf16[512,128]{1,0:T(8,128)(2,1)} %copy-done.21) | copy-start | bytes 393220
where the time goes:
time: 246 us; the launch traced here: 245 us
  starting transfers between devices  109 us (44%)
  waiting for transfers between devices  103 us (42%)
  Pallas kernels  22.7 us (9%)
  local copies, waits for them, and re-layouts  9.6 us (4%)
    ppermute x13, waiting for transfers between devices, shifted(): lax.ppermute(value, axis, [(i, (i + step) % size) for i in range(size)])  67.6 us
    all_to_all x2, starting transfers between devices, exchanged(): lax.all_to_all(parts, 'seq', split_axis=0, concat_axis=0, tiled=True)  53.1 us
    ppermute x13, starting transfers between devices, shifted(): lax.ppermute(value, axis, [(i, (i + step) % size) for i in range(size)])  52.1 us
    all_to_all x2, waiting for transfers between devices, exchanged(): lax.all_to_all(parts, 'seq', split_axis=0, concat_axis=0, tiled=True)  35.2 us
    pallas_call x10, Pallas kernels, run(): pl.pallas_call(body, out_shape=shapes if many else shapes[0], in_specs=sp...  22.7 us
    unnamed x46, local copies, waits for them, and re-layouts  8.41 us
  transfers between devices with their start and end apart: 16, of which 9 were waited for; matrix products, arithmetic and copies ran while one was open for 0% of the time, Pallas kernels for 8%

commit v1 on v0

--- a/solution.py
+++ b/solution.py
@@ -63,18 +63,26 @@
     return jax.ShapeDtypeStruct(dims, dtype)
 
 
-def pack_weights_body(up, bias, down, out):
+def pack_weights_body(side, up, bias, down, main, rest):
     hidden, width = up.shape
-    out[:hidden, :] = up[...]
-    row = bias[...]
-    high = row.astype(BF)
-    low = (row - high.astype(F32)).astype(BF)
-    slab = jnp.concatenate(
-        [high.astype(F32), low.astype(F32), jnp.zeros((ROWS - 2, hidden), F32)], axis=0
-    )
-    slab = jnp.concatenate([slab, jnp.zeros((ROWS, width - hidden), F32)], axis=1)
-    out[hidden : hidden + ROWS, :] = slab.astype(BF)
-    out[hidden + ROWS :, :] = down[...]
+    half = hidden // 2
+    for p in range(2):
+        first, second = slice(p * half, (p + 1) * half), slice((1 - p) * half, (2 - p) * half)
+
+        @pl.when(side[0] == p)
+        def _(first=first, second=second):
+            main[:half, :] = up[first, :]
+            main[half:hidden, :] = up[second, :]
+            row = jnp.concatenate([bias[:, first], bias[:, second]], axis=1)
+            top = row.astype(BF)
+            low = (row - top.astype(F32)).astype(BF)
+            slab = jnp.concatenate(
+                [top.astype(F32), low.astype(F32), jnp.zeros((ROWS - 2, hidden), F32)], axis=0
+            )
+            slab = jnp.concatenate([slab, jnp.zeros((ROWS, width - hidden), F32)], axis=1)
+            main[hidden : hidden + ROWS, :] = slab.astype(BF)
+            main[hidden + ROWS :, :] = down[first, :]
+            rest[...] = down[second, :]
 
 
 def dispatch_body(number, capacity, ids, gates, tokens, buffer, high, low):
@@ -160,33 +168,43 @@
     return slab[0:1, :].astype(F32) + slab[1:2, :].astype(F32)
 
 
-def steps_body(pieces, rows, *refs):
+def steps_body(pieces, others, rows, *refs):
     *ins, total, ups, downs = refs
-    hidden = (ins[0].shape[0] - ROWS) // 2
+    mains, rests = ins[:pieces], ins[pieces : pieces + others]
+    half = (mains[0].shape[0] - ROWS) // 3
+    hidden = 2 * half
     slabs = []
-    for k, piece in enumerate(ins[:pieces]):
+    for k, main in enumerate(mains):
         at = k * hidden
-        ups[at : at + hidden, :] = piece[:hidden, :]
-        downs[at : at + hidden, :] = piece[hidden + ROWS :, :]
-        slabs.append(bias_of(piece[hidden : hidden + ROWS, :hidden]))
+        ups[at : at + hidden, :] = main[:hidden, :]
+        downs[at : at + half, :] = main[hidden + ROWS :, :]
+        slabs.append(bias_of(main[hidden : hidden + ROWS, :hidden]))
+    at = half
+    for rest in rests:
+        for low in range(0, rest.shape[0], half):
+            downs[at : at + half, :] = rest[low : low + half, :]
+            at += hidden
     bias = jnp.concatenate(slabs, axis=1)
     count = rows.shape[0]
     size = count // 4
     for at in range(0, count, size):
         part = contribution(rows[at : at + size, :], ups[...], bias, downs[...])
-        if len(ins) > pieces:
-            part += ins[pieces][at : at + size, :]
+        if len(ins) > pieces + others:
+            part += ins[-1][at : at + size, :]
         total[at : at + size, :] = part
 
 
-def last_body(rows, upper, lower, old, own, other):
-    hidden = lower.shape[0]
+def last_body(rows, upper, lower, rest, old, own, other, down):
+    half = lower.shape[0]
+    hidden = 2 * half
+    down[:half, :] = lower[...]
+    down[half:, :] = rest[...]
     total = old[...] + contribution(
-        rows[...], upper[:hidden, :], bias_of(upper[hidden:, :hidden]), lower[...]
-    )
-    half = own.shape[0]
-    own[...] = total[:half]
-    other[...] = total[half:].astype(BF)
+        rows[...], upper[:hidden, :], bias_of(upper[hidden:, :hidden]), down[...]
+    )
+    count = own.shape[0]
+    own[...] = total[:count]
+    other[...] = total[count:].astype(BF)
 
 
 def reduce_body(own, other, bias, buffer):
@@ -273,22 +291,36 @@
     ring = lax.axis_size("exp")
     work = 8 * slots * width * hidden
 
-    own_piece = call(
-        pack_weights_body, shape((2 * hidden + ROWS, width), BF), 1 << 28
-    )(up_weight[0].T, up_bias, down_weight[0])
-    passed = [(shifted(own_piece, "exp", 1), shifted(own_piece, "exp", -1))]
-    for _ in range(2, ring // 2):
+    half = hidden // 2
+    side = (lax.axis_index("groups") % 2).astype(jnp.int32).reshape(1)
+    own_main, own_rest = call(
+        pack_weights_body,
+        [shape((hidden + ROWS + half, width), BF), shape((half, width), BF)],
+        1 << 24,
+        smem=(0,),
+    )(side, up_weight[0].T, up_bias, down_weight[0])
+
+    def twin_of(value):
+        return lax.ppermute(value, "groups", [(i, i ^ 1) for i in range(lax.axis_size("groups"))])
+
+    passed, rests = [(own_main, own_main)], [own_rest]
+    for _ in range(1, ring // 2):
         right, left = passed[-1]
-        passed.append((shifted(right, "exp", 1), shifted(left, "exp", -1)))
+        right, left = shifted(right, "exp", 1), shifted(left, "exp", -1)
+        both = jnp.concatenate([right[hidden + ROWS :], left[hidden + ROWS :]], axis=0)
+        rests.append(twin_of(both))
+        passed.append((right, left))
+    lower = shifted(passed[-1][1][hidden + ROWS :], "exp", -1)
+    upper = shifted(passed[-1][0][: hidden + ROWS], "exp", 1)
+    last_rest = twin_of(lower)
 
     own_kv = call(select_body, shape((2 * attn_query.shape[1], length), BF), 1 << 24, smem=(0,))(
         block_flags, fresh_keys.T, fresh_values.T, stale_keys.T, stale_values.T
     )
     size = lax.axis_size("seq")
     near = math.gcd(size, 4)
-    far_kv = jnp.concatenate(
-        [own_kv] + [shifted(own_kv, "seq", near * k) for k in range(1, size // near)], axis=0
-    )
+    far_kv = [own_kv] + [shifted(own_kv, "seq", near * k) for k in range(1, size // near)]
+    far_kv = jnp.concatenate(far_kv, axis=0)
 
     buffer, high, low = call(
         functools.partial(dispatch_body, number, capacity),
@@ -302,7 +334,7 @@
         return moved.reshape(packed)
 
     received = exchanged(buffer)
-    received = after(received, passed[1])
+    received = after(received, passed[2])
 
     runs = [[near * a + b for b in range(near)] for a in range(size // near)]
     gathered = to_each(after(far_kv, received), "seq", runs)
@@ -311,25 +343,25 @@
         received, shifted(received, "tp", 1)
     )
 
-    def steps(pieces, old=None):
+    def steps(mains, others, old=None):
         extra = [] if old is None else [old]
-        both = pltpu.VMEM((len(pieces) * hidden, width), BF)
+        joined = pltpu.VMEM((len(mains) * hidden, width), BF)
         return call(
-            functools.partial(steps_body, len(pieces)),
+            functools.partial(steps_body, len(mains), len(others)),
             shape((2 * slots, width), F32),
-            len(pieces) * work,
-            aliases={len(pieces) + 1: 0} if extra else None,
-            scratch=(both, both),
-        )(rows, *pieces, *extra)
-
-    early = steps([own_piece] + [p for pair in passed[:-1] for p in pair])
-    total = steps(list(passed[-1]), early)
-    right, left = after(passed[-1], early, far_kv)
-    upper = shifted(right[: hidden + ROWS], "exp", 1)
-    lower = shifted(left[hidden + ROWS :], "exp", -1)
+            len(mains) * work,
+            aliases={len(mains) + len(others) + 1: 0} if extra else None,
+            scratch=(joined, joined),
+        )(rows, *mains, *others, *extra)
+
+    early = steps([own_main] + [p for pair in passed[1:-1] for p in pair], rests[:-1])
+    total = steps(list(passed[-1]), rests[-1:], early)
     own, other = call(
-        last_body, [shape((slots, width), F32), shape((slots, width), BF)], work
-    )(rows, upper, lower, total)
+        last_body,
+        [shape((slots, width), F32), shape((slots, width), BF)],
+        work,
+        scratch=(pltpu.VMEM((hidden, width), BF),),
+    )(rows, upper, lower, last_rest, total)
     result = call(reduce_body, shape(packed, BF), 1 << 28)(own, shifted(other, "tp", 1), down_bias)
     back = exchanged(after(result, gathered))
     attn_out = call(attend_body, shape(attn_query.shape[::-1], BF), 1 << 31)(attn_query.T, gathered)

time: 246 us -> 239 us (0.972)
  the two profiles are of different devices: /device:TPU:68 before, /device:TPU:70 now
where the time goes in v1:
time: 239 us; the launch traced here: 237 us
  starting transfers between devices  125 us (52%)
  waiting for transfers between devices  81.3 us (34%)
  Pallas kernels  22.5 us (9%)
  local copies, waits for them, and re-layouts  7.72 us (3%)
    all_to_all x2, starting transfers between devices, exchanged(): lax.all_to_all(parts, 'seq', split_axis=0, concat_axis=0, tiled=True)  53.2 us
    ppermute x13, starting transfers between devices, shifted(): lax.ppermute(value, axis, [(i, (i + step) % size) for i in range(size)])  51.6 us
    ppermute x13, waiting for transfers between devices, shifted(): lax.ppermute(value, axis, [(i, (i + step) % size) for i in range(size)])  42.5 us
    all_to_all x2, waiting for transfers between devices, exchanged(): lax.all_to_all(parts, 'seq', split_axis=0, concat_axis=0, tiled=True)  35.3 us
    pallas_call x10, Pallas kernels, run(): pl.pallas_call(body, out_shape=shapes if many else shapes[0], in_specs=sp...  22.5 us
    ppermute x4, starting transfers between devices, twin_of(): lax.ppermute(value, 'groups', [(i, i ^ 1) for i in range(lax.axis_size('g...  16.3 us
  transfers between devices with their start and end apart: 20, of which 9 were waited for; matrix products, arithmetic and copies ran while one was open for 1% of the time, Pallas kernels for 8%

profile of v1, /device:TPU:70, one launch (start us, length us, event | category | flops | bytes accessed | tf_op | source)
XLA Modules:
  0.0 237.5 jit_solution(17121105399578246518)
XLA Ops:
  0.7 1.1 copy-done.15
  1.7 0.7 copy-done.17
  2.4 0.7 copy-done.18
  3.1 1.5 shard_map.141
  4.6 43.8 %all-to-all-start = ((bf16[16,8,2944]{2,1,0:T(8,128)(2,1)}), bf16[16,8,2944]{2,1,0:T(8,128)(2,1)S(1)}, u32[]{:S(2)}, u32[]{:S(2)}) async-start(bf16[16,8,2944]{2,1,0:T(8,128)(2,1)} %bitcast.7), calls=%async_computation | async-start | bytes 1507328 | tf_op jit(solution)/shard_map/all_to_all | solution.py:333
  48.5 0.1 shard_map.142
  48.6 4.8 %collective-permute-start.3 = (bf16[440,1152]{1,0:T(8,128)(2,1)S(1)}, bf16[440,1152]{1,0:T(8,128)(2,1)S(1)}, u32[]{:S(2)}, u32[]{:S(2)}) collective-permute-start(bf16[440,1152]{1,0:T(8,128)(2,1)S(1)} %get-tuple-element.13.refs_0_), channel_id=1, source_target_pairs={{0,2},{2,4},{4,6},{6,8},{8,10},{10,12},{12,14},{14,0},{1,3},{3,5},... | collective-permute-start | bytes 3041288 | tf_op jit(solution)/shard_map/ppermute | solution.py:21
  53.4 2.0 collective-permute-start.5
  55.3 1.0 copy-done.13
  56.3 18.5 %collective-permute-done.3.refs_1_ = bf16[440,1152]{1,0:T(8,128)(2,1)S(1)} collective-permute-done((bf16[440,1152]{1,0:T(8,128)(2,1)S(1)}, bf16[440,1152]{1,0:T(8,128)(2,1)S(1)}, u32[]{:S(2)}, u32[]{:S(2)}) %collective-permute-start.3) | collective-permute-done | bytes 1013792 | tf_op jit(solution)/shard_map/ppermute | solution.py:21
  74.8 5.6 %collective-permute-start.4 = (bf16[440,1152]{1,0:T(8,128)(2,1)S(1)}, bf16[440,1152]{1,0:T(8,128)(2,1)S(1)}, u32[]{:S(2)}, u32[]{:S(2)}) collective-permute-start(bf16[440,1152]{1,0:T(8,128)(2,1)S(1)} %collective-permute-done.3.refs_1_), channel_id=1, source_target_pairs={{0,2},{2,4},{4,6},{6,8},{8,10},{10,12},{12,14},{14,0},{1,3},{3,5},... | collective-permute-start | bytes 3041288 | tf_op jit(solution)/shard_map/ppermute | solution.py:21
  80.4 2.0 collective-permute-start.6
  82.5 0.6 shard_map.140
  83.0 7.3 %collective-permute-start = (bf16[144,256]{1,0:T(8,128)(2,1)S(1)}, bf16[144,256]{1,0:T(8,128)(2,1)S(1)}, u32[]{:S(2)}, u32[]{:S(2)}) collective-permute-start(bf16[144,256]{1,0:T(8,128)(2,1)S(1)} %shard_map.140), channel_id=1, source_target_pairs={{0,64},{16,80},{32,96},{48,112},{64,128},{80,144},{96,160},{112,17... | collective-permute-start | bytes 221192 | tf_op jit(solution)/shard_map/ppermute | solution.py:21
  90.3 7.3 %collective-permute-start.1 = (bf16[144,256]{1,0:T(8,128)(2,1)S(1)}, bf16[144,256]{1,0:T(8,128)(2,1)S(1)}, u32[]{:S(2)}, u32[]{:S(2)}) collective-permute-start(bf16[144,256]{1,0:T(8,128)(2,1)S(1)} %shard_map.140), channel_id=1, source_target_pairs={{0,128},{16,144},{32,160},{48,176},{64,192},{80,208},{96,224},{112... | collective-permute-start | bytes 221192 | tf_op jit(solution)/shard_map/ppermute | solution.py:21
  97.6 7.3 %collective-permute-start.2 = (bf16[144,256]{1,0:T(8,128)(2,1)S(1)}, bf16[144,256]{1,0:T(8,128)(2,1)S(1)}, u32[]{:S(2)}, u32[]{:S(2)}) collective-permute-start(bf16[144,256]{1,0:T(8,128)(2,1)S(1)} %shard_map.140), channel_id=1, source_target_pairs={{0,192},{16,208},{32,224},{48,240},{64,0},{80,16},{96,32},{112,48}... | collective-permute-start | bytes 221192 | tf_op jit(solution)/shard_map/ppermute | solution.py:21
  105.0 1.6 collective-permute-done.1
  106.5 5.8 %collective-permute-done.2 = bf16[144,256]{1,0:T(8,128)(2,1)S(1)} collective-permute-done((bf16[144,256]{1,0:T(8,128)(2,1)S(1)}, bf16[144,256]{1,0:T(8,128)(2,1)S(1)}, u32[]{:S(2)}, u32[]{:S(2)}) %collective-permute-start.2) | collective-permute-done | bytes 73760 | tf_op jit(solution)/shard_map/ppermute | solution.py:21
  112.4 1.0 copy-done.4
  113.4 1.1 broadcast_in_dim.2
  114.5 3.6 %all-to-all-start.1 = ((bf16[4,576,256]{2,1,0:T(8,128)(2,1)}), bf16[4,576,256]{2,1,0:T(8,128)(2,1)S(1)}, u32[]{:S(2)}, u32[]{:S(2)}) async-start(bf16[4,576,256]{2,1,0:T(8,128)(2,1)} %broadcast_in_dim.2), calls=%async_computation.1 | async-start | bytes 2359296 | tf_op jit(solution)/shard_map/all_to_all | solution.py:30
  118.1 2.1 collective-permute-start.10
  120.2 5.2 %collective-permute-start.8 = (bf16[440,1152]{1,0:T(8,128)(2,1)}, bf16[440,1152]{1,0:T(8,128)(2,1)S(1)}, u32[]{:S(2)}, u32[]{:S(2)}) collective-permute-start(bf16[440,1152]{1,0:T(8,128)(2,1)} %copy-done.4), channel_id=1, source_target_pairs={{0,2},{2,4},{4,6},{6,8},{8,10},{10,12},{12,14},{14,0},{1,3},{3,5},... | collective-permute-start | bytes 3041288 | tf_op jit(solution)/shard_map/ppermute | solution.py:21
  125.4 1.0 slice.33
  126.4 0.1 pad_maximum_fusion.1
  126.5 4.7 %collective-permute-start.14 = (bf16[288,1152]{1,0:T(8,128)(2,1)S(1)}, bf16[288,1152]{1,0:T(8,128)(2,1)S(1)}, u32[]{:S(2)}, u32[]{:S(2)}) collective-permute-start(bf16[288,1152]{1,0:T(8,128)(2,1)S(1)} %pad_maximum_fusion.1), channel_id=1, source_target_pairs={{0,256},{256,0},{1,257},{257,1},{2,258},{258,2},{3,259},{259,3},{4... | collective-permute-start | bytes 1990664 | tf_op jit(solution)/shard_map/ppermute | solution.py:304
  131.3 1.0 slice.35
  132.3 2.0 collective-permute-start.7
  134.3 2.0 collective-permute-start.15
  136.3 9.5 %collective-permute-done.10.refs_1_ = bf16[440,1152]{1,0:T(8,128)(2,1)S(1)} collective-permute-done((bf16[440,1152]{1,0:T(8,128)(2,1)}, bf16[440,1152]{1,0:T(8,128)(2,1)S(1)}, u32[]{:S(2)}, u32[]{:S(2)}) %collective-permute-start.10) | collective-permute-done | bytes 1013792 | tf_op jit(solution)/shard_map/ppermute | solution.py:21
  145.8 2.0 collective-permute-start.11
  147.8 4.7 %collective-permute-start.13 = (bf16[288,1152]{1,0:T(8,128)(2,1)S(1)}, bf16[288,1152]{1,0:T(8,128)(2,1)S(1)}, u32[]{:S(2)}, u32[]{:S(2)}) collective-permute-start(bf16[288,1152]{1,0:T(8,128)(2,1)S(1)} %pad_maximum_fusion), channel_id=1, source_target_pairs={{0,256},{256,0},{1,257},{257,1},{2,258},{258,2},{3,259},{259,3},{4... | collective-permute-start | bytes 1990664 | tf_op jit(solution)/shard_map/ppermute | solution.py:304
  152.7 4.9 %collective-permute-done.11.lower = bf16[144,1152]{1,0:T(8,128)(2,1)S(1)} collective-permute-done((bf16[144,1152]{1,0:T(8,128)(2,1)S(1)}, bf16[144,1152]{1,0:T(8,128)(2,1)S(1)}, u32[]{:S(2)}, u32[]{:S(2)}) %collective-permute-start.11) | collective-permute-done | bytes 331808 | tf_op jit(solution)/shard_map/ppermute | solution.py:21
  157.6 2.3 collective-permute-start.9
  159.9 4.9 %collective-permute-start.12 = (bf16[144,1152]{1,0:T(8,128)(2,1)S(1)}, bf16[144,1152]{1,0:T(8,128)(2,1)S(1)}, u32[]{:S(2)}, u32[]{:S(2)}) collective-permute-start(bf16[144,1152]{1,0:T(8,128)(2,1)S(1)} %collective-permute-done.11.lower), channel_id=1, source_target_pairs={{0,256},{256,0},{1,257},{257,1},{2,258},{258,2},{3,259},{259,3},{4... | collective-permute-start | bytes 995336 | tf_op jit(solution)/shard_map/ppermute | solution.py:304
  164.8 0.4 shard_map.144.rows
  165.2 8.2 %shard_map.145.refs_3_ = f32[640,1152]{1,0:T(8,128)S(1)} custom-call(bf16[640,1152]{1,0:T(8,128)(2,1)S(1)} %shard_map.144.rows, bf16[440,1152]{1,0:T(8,128)(2,1)S(1)} %copy-done.14, bf16[440,1152]{1,0:T(8,128)(2,1)S(1)} %collective-permute-done.3.refs_1_, bf16[440,1152]{1,0:T(8,128)(2,1)S(1)} %copy-done.3, bf16[440,1152]{1,0:T(8,128)(2,1)S(1)} %copy-done.5, ...), custom_call_target="tpu_custom_call" | custom-call | flops 4246732800 | bytes 11151360 | tf_op jit(solution)/shard_map/pallas_call | solution.py:48
  173.5 1.9 collective-permute-done.13.refs_2_
  175.4 4.1 %shard_map.146.old = f32[640,1152]{1,0:T(8,128)S(1)} custom-call(bf16[640,1152]{1,0:T(8,128)(2,1)S(1)} %shard_map.144.rows, bf16[440,1152]{1,0:T(8,128)(2,1)S(1)} %collective-permute-done.8.refs_0_, bf16[440,1152]{1,0:T(8,128)(2,1)S(1)} %collective-permute-done.10.refs_1_, ...), custom_call_target="tpu_custom_call", output_to_operand_aliasing={{}: (4, {})} | custom-call | flops 1698693120 | bytes 10063872 | tf_op jit(solution)/shard_map/pallas_call | solution.py:48
  179.5 1.6 collective-permute-done.12.rest
  181.1 2.0 shard_map.147
  183.1 2.0 collective-permute-start.16
  185.1 2.2 collective-permute-done.16.other
  187.3 1.5 shard_map.148
  188.8 9.3 %all-to-all-start.2 = ((bf16[16,8,2944]{2,1,0:T(8,128)(2,1)}), bf16[16,8,2944]{2,1,0:T(8,128)(2,1)S(1)}, u32[]{:S(2)}, u32[]{:S(2)}) async-start(bf16[16,8,2944]{2,1,0:T(8,128)(2,1)} %bitcast.15), calls=%async_computation.2 | async-start | bytes 1507328 | tf_op jit(solution)/shard_map/all_to_all | solution.py:333
  198.1 2.8 %shard_map.143 = bf16[72,256]{1,0:T(8,128)(2,1)} custom-call(bf16[72,256]{1,0:T(8,128)(2,1)S(1)} %bitcast.28, bf16[2304,256]{1,0:T(8,128)(2,1)S(1)} %bitcast.20), custom_call_target="tpu_custom_call" | custom-call | flops 2147483648 | bytes 1253376 | tf_op jit(solution)/shard_map/pallas_call | solution.py:48
  200.9 35.3 %all-to-all-done.2 = bf16[16,8,2944]{2,1,0:T(8,128)(2,1)S(1)} async-done(((bf16[16,8,2944]{2,1,0:T(8,128)(2,1)}), bf16[16,8,2944]{2,1,0:T(8,128)(2,1)S(1)}, u32[]{:S(2)}, u32[]{:S(2)}) %all-to-all-start.2) | async-done | bytes 753696 | tf_op jit(solution)/shard_map/all_to_all | solution.py:333
  236.1 1.4 shard_map.149
  (52 shorter events, 0.4 us)
Async XLA Ops:
  0.6 47.8 %copy-start = (bf16[1,1152,288]{1,2,0:T(8,128)(2,1)S(1)}, bf16[1,1152,288]{1,2,0:T(8,128)(2,1)}, u32[]{:S(2)}) copy-start(bf16[1,1152,288]{1,2,0:T(8,128)(2,1)} %param.22) | copy-start | bytes 1990660
  0.6 47.8 %copy-start.1 = (bf16[1,288,1152]{2,1,0:T(8,128)(2,1)S(1)}, bf16[1,288,1152]{2,1,0:T(8,128)(2,1)}, u32[]{:S(2)}) copy-start(bf16[1,288,1152]{2,1,0:T(8,128)(2,1)} %param.24) | copy-start | bytes 1990660
  0.7 47.8 %copy-start.11 = (f32[1,288]{1,0:T(1,128)S(1)}, f32[1,288]{1,0:T(1,128)}, u32[]{:S(2)}) copy-start(f32[1,288]{1,0:T(1,128)} %bias.2) | copy-start | bytes 3460
  0.7 1.1 copy-start.15
  1.7 0.7 copy-start.17
  2.4 0.7 copy-start.18
  4.6 77.8 %copy-start.6 = (bf16[256,72]{0,1:T(8,128)(2,1)S(1)}, bf16[256,72]{0,1:T(8,128)(2,1)}, u32[]{:S(2)}) copy-start(bf16[256,72]{0,1:T(8,128)(2,1)} %param.14) | copy-start | bytes 110596
  4.6 77.9 %copy-start.7 = (bf16[256,72]{0,1:T(8,128)(2,1)S(1)}, bf16[256,72]{0,1:T(8,128)(2,1)}, u32[]{:S(2)}) copy-start(bf16[256,72]{0,1:T(8,128)(2,1)} %param.15) | copy-start | bytes 110596
  4.6 77.9 %copy-start.8 = (bf16[256,72]{0,1:T(8,128)(2,1)S(1)}, bf16[256,72]{0,1:T(8,128)(2,1)}, u32[]{:S(2)}) copy-start(bf16[256,72]{0,1:T(8,128)(2,1)} %param.16) | copy-start | bytes 110596
  4.6 77.9 %copy-start.9 = (bf16[256,72]{0,1:T(8,128)(2,1)S(1)}, bf16[256,72]{0,1:T(8,128)(2,1)}, u32[]{:S(2)}) copy-start(bf16[256,72]{0,1:T(8,128)(2,1)} %param.17) | copy-start | bytes 110596
  4.6 77.9 %copy-start.12 = (s32[2]{0:T(128)S(1)}, s32[2]{0:T(128)}, u32[]{:S(2)}) copy-start(s32[2]{0:T(128)} %flags.1) | copy-start | bytes 28
  4.6 108.8 %all-to-all-start = ((bf16[16,8,2944]{2,1,0:T(8,128)(2,1)}), bf16[16,8,2944]{2,1,0:T(8,128)(2,1)S(1)}, u32[]{:S(2)}, u32[]{:S(2)}) async-start(bf16[16,8,2944]{2,1,0:T(8,128)(2,1)} %bitcast.7), calls=%async_computation | async-start | bytes 1507328 | tf_op jit(solution)/shard_map/all_to_all | solution.py:333
  48.6 26.2 %collective-permute-start.3 = (bf16[440,1152]{1,0:T(8,128)(2,1)S(1)}, bf16[440,1152]{1,0:T(8,128)(2,1)S(1)}, u32[]{:S(2)}, u32[]{:S(2)}) collective-permute-start(bf16[440,1152]{1,0:T(8,128)(2,1)S(1)} %get-tuple-element.13.refs_0_), channel_id=1, source_target_pairs={{0,2},{2,4},{4,6},{6,8},{8,10},{10,12},{12,14},{14,0},{1,3},{3,5},... | collective-permute-start | bytes 3041288 | tf_op jit(solution)/shard_map/ppermute | solution.py:21
  53.4 27.1 %collective-permute-start.5 = (bf16[440,1152]{1,0:T(8,128)(2,1)S(1)}, bf16[440,1152]{1,0:T(8,128)(2,1)S(1)}, u32[]{:S(2)}, u32[]{:S(2)}) collective-permute-start(bf16[440,1152]{1,0:T(8,128)(2,1)S(1)} %get-tuple-element.13.refs_0_), channel_id=1, source_target_pairs={{0,14},{2,0},{4,2},{6,4},{8,6},{10,8},{12,10},{14,12},{1,15},{3,1}... | collective-permute-start | bytes 3041288 | tf_op jit(solution)/shard_map/ppermute | solution.py:21
  55.3 1.0 copy-start.13
  74.8 37.6 %collective-permute-start.4 = (bf16[440,1152]{1,0:T(8,128)(2,1)S(1)}, bf16[440,1152]{1,0:T(8,128)(2,1)S(1)}, u32[]{:S(2)}, u32[]{:S(2)}) collective-permute-start(bf16[440,1152]{1,0:T(8,128)(2,1)S(1)} %collective-permute-done.3.refs_1_), channel_id=1, source_target_pairs={{0,2},{2,4},{4,6},{6,8},{8,10},{10,12},{12,14},{14,0},{1,3},{3,5},... | collective-permute-start | bytes 3041288 | tf_op jit(solution)/shard_map/ppermute | solution.py:21
  80.4 31.9 %copy-start.2 = (bf16[440,1152]{1,0:T(8,128)(2,1)}, bf16[440,1152]{1,0:T(8,128)(2,1)S(1)}, u32[]{:S(2)}) copy-start(bf16[440,1152]{1,0:T(8,128)(2,1)S(1)} %collective-permute-done.5.refs_2_) | copy-start | bytes 3041284
  80.4 32.9 %collective-permute-start.6 = (bf16[440,1152]{1,0:T(8,128)(2,1)S(1)}, bf16[440,1152]{1,0:T(8,128)(2,1)}, u32[]{:S(2)}, u32[]{:S(2)}) collective-permute-start(bf16[440,1152]{1,0:T(8,128)(2,1)S(1)} %collective-permute-done.5.refs_2_), channel_id=1, source_target_pairs={{0,14},{2,0},{4,2},{6,4},{8,6},{10,8},{12,10},{14,12},{1,15},{3,1}... | collective-permute-start | bytes 3041288 | tf_op jit(solution)/shard_map/ppermute | solution.py:21
  83.0 21.9 %collective-permute-start = (bf16[144,256]{1,0:T(8,128)(2,1)S(1)}, bf16[144,256]{1,0:T(8,128)(2,1)S(1)}, u32[]{:S(2)}, u32[]{:S(2)}) collective-permute-start(bf16[144,256]{1,0:T(8,128)(2,1)S(1)} %shard_map.140), channel_id=1, source_target_pairs={{0,64},{16,80},{32,96},{48,112},{64,128},{80,144},{96,160},{112,17... | collective-permute-start | bytes 221192 | tf_op jit(solution)/shard_map/ppermute | solution.py:21
  90.3 16.2 %collective-permute-start.1 = (bf16[144,256]{1,0:T(8,128)(2,1)S(1)}, bf16[144,256]{1,0:T(8,128)(2,1)S(1)}, u32[]{:S(2)}, u32[]{:S(2)}) collective-permute-start(bf16[144,256]{1,0:T(8,128)(2,1)S(1)} %shard_map.140), channel_id=1, source_target_pairs={{0,128},{16,144},{32,160},{48,176},{64,192},{80,208},{96,224},{112... | collective-permute-start | bytes 221192 | tf_op jit(solution)/shard_map/ppermute | solution.py:21
  97.6 14.7 %collective-permute-start.2 = (bf16[144,256]{1,0:T(8,128)(2,1)S(1)}, bf16[144,256]{1,0:T(8,128)(2,1)S(1)}, u32[]{:S(2)}, u32[]{:S(2)}) collective-permute-start(bf16[144,256]{1,0:T(8,128)(2,1)S(1)} %shard_map.140), channel_id=1, source_target_pairs={{0,192},{16,208},{32,224},{48,240},{64,0},{80,16},{96,32},{112,48}... | collective-permute-start | bytes 221192 | tf_op jit(solution)/shard_map/ppermute | solution.py:21
  112.4 1.0 copy-start.4
  114.5 74.3 %all-to-all-start.1 = ((bf16[4,576,256]{2,1,0:T(8,128)(2,1)}), bf16[4,576,256]{2,1,0:T(8,128)(2,1)S(1)}, u32[]{:S(2)}, u32[]{:S(2)}) async-start(bf16[4,576,256]{2,1,0:T(8,128)(2,1)} %broadcast_in_dim.2), calls=%async_computation.1 | async-start | bytes 2359296 | tf_op jit(solution)/shard_map/all_to_all | solution.py:30
  118.1 13.1 %copy-start.5 = (bf16[440,1152]{1,0:T(8,128)(2,1)S(1)}, bf16[440,1152]{1,0:T(8,128)(2,1)}, u32[]{:S(2)}) copy-start(bf16[440,1152]{1,0:T(8,128)(2,1)} %copy-done.4) | copy-start | bytes 3041284
  118.1 27.6 %collective-permute-start.10 = (bf16[440,1152]{1,0:T(8,128)(2,1)}, bf16[440,1152]{1,0:T(8,128)(2,1)S(1)}, u32[]{:S(2)}, u32[]{:S(2)}) collective-permute-start(bf16[440,1152]{1,0:T(8,128)(2,1)} %collective-permute-done.6.refs_4_), channel_id=1, source_target_pairs={{0,14},{2,0},{4,2},{6,4},{8,6},{10,8},{12,10},{14,12},{1,15},{3,1}... | collective-permute-start | bytes 3041288 | tf_op jit(solution)/shard_map/ppermute | solution.py:21
  120.2 27.5 %collective-permute-start.8 = (bf16[440,1152]{1,0:T(8,128)(2,1)}, bf16[440,1152]{1,0:T(8,128)(2,1)S(1)}, u32[]{:S(2)}, u32[]{:S(2)}) collective-permute-start(bf16[440,1152]{1,0:T(8,128)(2,1)} %copy-done.4), channel_id=1, source_target_pairs={{0,2},{2,4},{4,6},{6,8},{8,10},{10,12},{12,14},{14,0},{1,3},{3,5},... | collective-permute-start | bytes 3041288 | tf_op jit(solution)/shard_map/ppermute | solution.py:21
  126.5 38.7 %collective-permute-start.14 = (bf16[288,1152]{1,0:T(8,128)(2,1)S(1)}, bf16[288,1152]{1,0:T(8,128)(2,1)S(1)}, u32[]{:S(2)}, u32[]{:S(2)}) collective-permute-start(bf16[288,1152]{1,0:T(8,128)(2,1)S(1)} %pad_maximum_fusion.1), channel_id=1, source_target_pairs={{0,256},{256,0},{1,257},{257,1},{2,258},{258,2},{3,259},{259,3},{4... | collective-permute-start | bytes 1990664 | tf_op jit(solution)/shard_map/ppermute | solution.py:304
  132.3 27.6 %collective-permute-start.7 = (bf16[128,2944]{1,0:T(8,128)(2,1)S(1)}, bf16[128,2944]{1,0:T(8,128)(2,1)S(1)}, u32[]{:S(2)}, u32[]{:S(2)}) collective-permute-start(bf16[128,2944]{1,0:T(8,128)(2,1)S(1)} %bitcast.18), channel_id=1, source_target_pairs={{0,1},{1,0},{2,3},{3,2},{4,5},{5,4},{6,7},{7,6},{8,9},{9,8},{10,11... | collective-permute-start | bytes 2261000 | tf_op jit(solution)/shard_map/ppermute | solution.py:21
  134.3 30.9 %collective-permute-start.15 = (bf16[288,1152]{1,0:T(8,128)(2,1)S(1)}, bf16[288,1152]{1,0:T(8,128)(2,1)S(1)}, u32[]{:S(2)}, u32[]{:S(2)}) collective-permute-start(bf16[288,1152]{1,0:T(8,128)(2,1)S(1)} %pad_maximum_fusion.2), channel_id=1, source_target_pairs={{0,256},{256,0},{1,257},{257,1},{2,258},{258,2},{3,259},{259,3},{4... | collective-permute-start | bytes 1990664 | tf_op jit(solution)/shard_map/ppermute | solution.py:304
  145.8 11.8 %collective-permute-start.11 = (bf16[144,1152]{1,0:T(8,128)(2,1)S(1)}, bf16[144,1152]{1,0:T(8,128)(2,1)S(1)}, u32[]{:S(2)}, u32[]{:S(2)}) collective-permute-start(bf16[144,1152]{1,0:T(8,128)(2,1)S(1)} %slice.30), channel_id=1, source_target_pairs={{0,14},{2,0},{4,2},{6,4},{8,6},{10,8},{12,10},{14,12},{1,15},{3,1}... | collective-permute-start | bytes 995336 | tf_op jit(solution)/shard_map/ppermute | solution.py:21
  147.8 27.6 %collective-permute-start.13 = (bf16[288,1152]{1,0:T(8,128)(2,1)S(1)}, bf16[288,1152]{1,0:T(8,128)(2,1)S(1)}, u32[]{:S(2)}, u32[]{:S(2)}) collective-permute-start(bf16[288,1152]{1,0:T(8,128)(2,1)S(1)} %pad_maximum_fusion), channel_id=1, source_target_pairs={{0,256},{256,0},{1,257},{257,1},{2,258},{258,2},{3,259},{259,3},{4... | collective-permute-start | bytes 1990664 | tf_op jit(solution)/shard_map/ppermute | solution.py:304
  152.6 12.6 %copy-start.3 = (bf16[440,1152]{1,0:T(8,128)(2,1)S(1)}, bf16[440,1152]{1,0:T(8,128)(2,1)}, u32[]{:S(2)}) copy-start(bf16[440,1152]{1,0:T(8,128)(2,1)} %copy-done.2) | copy-start | bytes 3041284
  152.6 12.6 %copy-start.14 = (bf16[440,1152]{1,0:T(8,128)(2,1)S(1)}, bf16[440,1152]{1,0:T(8,128)(2,1)}, u32[]{:S(2)}) copy-start(bf16[440,1152]{1,0:T(8,128)(2,1)} %copy-done.13) | copy-start | bytes 3041284
  157.6 23.5 %collective-permute-start.9 = (bf16[296,1152]{1,0:T(8,128)(2,1)S(1)}, bf16[296,1152]{1,0:T(8,128)(2,1)S(1)}, u32[]{:S(2)}, u32[]{:S(2)}) collective-permute-start(bf16[296,1152]{1,0:T(8,128)(2,1)S(1)} %slice.29), channel_id=1, source_target_pairs={{0,2},{2,4},{4,6},{6,8},{8,10},{10,12},{12,14},{14,0},{1,3},{3,5},... | collective-permute-start | bytes 2045960 | tf_op jit(solution)/shard_map/ppermute | solution.py:21
  159.9 21.2 %collective-permute-start.12 = (bf16[144,1152]{1,0:T(8,128)(2,1)S(1)}, bf16[144,1152]{1,0:T(8,128)(2,1)S(1)}, u32[]{:S(2)}, u32[]{:S(2)}) collective-permute-start(bf16[144,1152]{1,0:T(8,128)(2,1)S(1)} %collective-permute-done.11.lower), channel_id=1, source_target_pairs={{0,256},{256,0},{1,257},{257,1},{2,258},{258,2},{3,259},{259,3},{4... | collective-permute-start | bytes 995336 | tf_op jit(solution)/shard_map/ppermute | solution.py:304
  179.5 7.8 %copy-start.10 = (f32[1,1152]{1,0:T(1,128)S(1)}, f32[1,1152]{1,0:T(1,128)}, u32[]{:S(2)}) copy-start(f32[1,1152]{1,0:T(1,128)} %bias.3) | copy-start | bytes 13828
  183.1 4.1 %collective-permute-start.16 = (bf16[320,1152]{1,0:T(8,128)(2,1)S(1)}, bf16[320,1152]{1,0:T(8,128)(2,1)S(1)}, u32[]{:S(2)}, u32[]{:S(2)}) collective-permute-start(bf16[320,1152]{1,0:T(8,128)(2,1)S(1)} %get-tuple-element.20), channel_id=1, source_target_pairs={{0,1},{1,0},{2,3},{3,2},{4,5},{5,4},{6,7},{7,6},{8,9},{9,8},{10,11... | collective-permute-start | bytes 2211848 | tf_op jit(solution)/shard_map/ppermute | solution.py:21
  188.8 9.3 %copy-start.16 = (bf16[256,72]{0,1:T(8,128)(2,1)S(1)}, bf16[256,72]{0,1:T(8,128)(2,1)}, u32[]{:S(2)}) copy-start(bf16[256,72]{0,1:T(8,128)(2,1)} %param.13) | copy-start | bytes 110596
  188.8 47.3 %all-to-all-start.2 = ((bf16[16,8,2944]{2,1,0:T(8,128)(2,1)}), bf16[16,8,2944]{2,1,0:T(8,128)(2,1)S(1)}, u32[]{:S(2)}, u32[]{:S(2)}) async-start(bf16[16,8,2944]{2,1,0:T(8,128)(2,1)} %bitcast.15), calls=%async_computation.2 | async-start | bytes 1507328 | tf_op jit(solution)/shard_map/all_to_all | solution.py:333

commit v2 on v1

--- a/solution.py
+++ b/solution.py
@@ -35,16 +35,18 @@
     return lax.dot_general(a, b, (((over_a,), (over_b,)), ((), ())), preferred_element_type=F32)
 
 
-def call(body, outs, flops, aliases=None, smem=(), scratch=()):
+def call(body, outs, flops, aliases=None, smem=(), scratch=(), away=()):
     def run(*args):
         specs = [
-            pl.BlockSpec(memory_space=pltpu.SMEM if i in smem else pltpu.VMEM)
+            pl.BlockSpec(
+                memory_space=pltpu.SMEM if i in smem else pl.ANY if i in away else pltpu.VMEM
+            )
             for i in range(len(args))
         ]
         many = isinstance(outs, (list, tuple))
         shapes = list(outs) if many else [outs]
         size = sum(math.prod(s.shape) * s.dtype.itemsize for s in (*args, *shapes))
-        out_specs = [pl.BlockSpec(memory_space=pltpu.VMEM) for _ in shapes]
+        out_specs = [pl.BlockSpec(memory_space=pl.ANY if away else pltpu.VMEM) for _ in shapes]
         return pl.pallas_call(
             body,
             out_shape=shapes if many else shapes[0],
@@ -63,26 +65,37 @@
     return jax.ShapeDtypeStruct(dims, dtype)
 
 
-def pack_weights_body(side, up, bias, down, main, rest):
+def pack_weights_body(side, up, bias, down, main, rest, slab, sems):
     hidden, width = up.shape
     half = hidden // 2
     for p in range(2):
-        first, second = slice(p * half, (p + 1) * half), slice((1 - p) * half, (2 - p) * half)
+        first, second = pl.ds(p * half, half), pl.ds((1 - p) * half, half)
 
         @pl.when(side[0] == p)
-        def _(first=first, second=second):
-            main[:half, :] = up[first, :]
-            main[half:hidden, :] = up[second, :]
-            row = jnp.concatenate([bias[:, first], bias[:, second]], axis=1)
+        def _(p=p, first=first, second=second):
+            moves = [
+                pltpu.make_async_copy(up.at[first], main.at[pl.ds(0, half)], sems.at[0]),
+                pltpu.make_async_copy(up.at[second], main.at[pl.ds(half, half)], sems.at[1]),
+                pltpu.make_async_copy(down.at[first], main.at[pl.ds(hidden + ROWS, half)], sems.at[2]),
+                pltpu.make_async_copy(down.at[second], rest, sems.at[3]),
+            ]
+            for move in moves:
+                move.start()
+            row = jnp.concatenate(
+                [bias[:, p * half : (p + 1) * half], bias[:, (1 - p) * half : (2 - p) * half]], axis=1
+            )
             top = row.astype(BF)
             low = (row - top.astype(F32)).astype(BF)
-            slab = jnp.concatenate(
+            lines = jnp.concatenate(
                 [top.astype(F32), low.astype(F32), jnp.zeros((ROWS - 2, hidden), F32)], axis=0
             )
-            slab = jnp.concatenate([slab, jnp.zeros((ROWS, width - hidden), F32)], axis=1)
-            main[hidden : hidden + ROWS, :] = slab.astype(BF)
-            main[hidden + ROWS :, :] = down[first, :]
-            rest[...] = down[second, :]
+            lines = jnp.concatenate([lines, jnp.zeros((ROWS, width - hidden), F32)], axis=1)
+            slab[...] = lines.astype(BF)
+            last = pltpu.make_async_copy(slab, main.at[pl.ds(hidden, ROWS)], sems.at[4])
+            last.start()
+            for move in moves:
+                move.wait()
+            last.wait()
 
 
 def dispatch_body(number, capacity, ids, gates, tokens, buffer, high, low):
@@ -194,6 +207,15 @@
         total[at : at + size, :] = part
 
 
+def join_body(right, left, out, *upper):
+    half = out.shape[0] // 2
+    keep = right.shape[0] - half
+    out[:half, :] = right[keep:, :]
+    out[half:, :] = left[keep:, :]
+    for ref in upper:
+        ref[...] = right[:keep, :]
+
+
 def last_body(rows, upper, lower, rest, old, own, other, down):
     half = lower.shape[0]
     hidden = 2 * half
@@ -298,20 +320,26 @@
         [shape((hidden + ROWS + half, width), BF), shape((half, width), BF)],
         1 << 24,
         smem=(0,),
+        scratch=(pltpu.VMEM((ROWS, width), BF), pltpu.SemaphoreType.DMA((5,))),
+        away=(1, 3),
     )(side, up_weight[0].T, up_bias, down_weight[0])
 
     def twin_of(value):
         return lax.ppermute(value, "groups", [(i, i ^ 1) for i in range(lax.axis_size("groups"))])
 
     passed, rests = [(own_main, own_main)], [own_rest]
-    for _ in range(1, ring // 2):
+    for step in range(1, ring // 2):
         right, left = passed[-1]
-        right, left = shifted(right, "exp", 1), shifted(left, "exp", -1)
-        both = jnp.concatenate([right[hidden + ROWS :], left[hidden + ROWS :]], axis=0)
+        right = shifted(right, "exp", 1)
+        left = shifted(left, "exp", -1)
+        outs = [shape((hidden, width), BF)]
+        if step == ring // 2 - 1:
+            outs.append(shape((hidden + ROWS, width), BF))
+        both, *top = call(join_body, outs, 1 << 20)(right, left)
         rests.append(twin_of(both))
         passed.append((right, left))
     lower = shifted(passed[-1][1][hidden + ROWS :], "exp", -1)
-    upper = shifted(passed[-1][0][: hidden + ROWS], "exp", 1)
+    upper = shifted(top[0], "exp", 1)
     last_rest = twin_of(lower)
 
     own_kv = call(select_body, shape((2 * attn_query.shape[1], length), BF), 1 << 24, smem=(0,))(

time: 239 us -> 244 us (1.021)
  waiting for transfers between devices: 81.3 us -> 84.2 us
    ppermute x4, waiting for transfers between devices: 3.52 us -> 7.05 us  [twin_of(): lax.ppermute(value, 'groups', [(i, i ^ 1) for i in range(lax.axis_size('g...]
    pallas_call x10 -> x13, Pallas kernels: 22.5 us -> 24.1 us  [run(): pl.pallas_call(body, out_shape=shapes if many else shapes[0], in_specs=sp...]
    unnamed x38 -> x40, local copies, waits for them, and re-layouts: 4.43 us -> 5.64 us
  transfers between devices with their start and end apart: 20 -> 20, of which waited for: 9 -> 9; matrix products, arithmetic and copies ran while one was open for 1% -> 0% of each run, Pallas kernels for 8% -> 9%
where the time goes in v2:
time: 244 us; the launch traced here: 243 us
  starting transfers between devices  125 us (51%)
  waiting for transfers between devices  84.2 us (35%)
  Pallas kernels  24.1 us (10%)
  local copies, waits for them, and re-layouts  7.73 us (3%)
    all_to_all x2, starting transfers between devices, exchanged(): lax.all_to_all(parts, 'seq', split_axis=0, concat_axis=0, tiled=True)  53.3 us
    ppermute x13, starting transfers between devices, shifted(): lax.ppermute(value, axis, [(i, (i + step) % size) for i in range(size)])  51.6 us
    ppermute x13, waiting for transfers between devices, shifted(): lax.ppermute(value, axis, [(i, (i + step) % size) for i in range(size)])  42 us
    all_to_all x2, waiting for transfers between devices, exchanged(): lax.all_to_all(parts, 'seq', split_axis=0, concat_axis=0, tiled=True)  35.2 us
    pallas_call x13, Pallas kernels, run(): pl.pallas_call(body, out_shape=shapes if many else shapes[0], in_specs=sp...  24.1 us
    ppermute x4, starting transfers between devices, twin_of(): lax.ppermute(value, 'groups', [(i, i ^ 1) for i in range(lax.axis_size('g...  16.6 us
    ppermute x4, waiting for transfers between devices, twin_of(): lax.ppermute(value, 'groups', [(i, i ^ 1) for i in range(lax.axis_size('g...  7.05 us
    unnamed x40, local copies, waits for them, and re-layouts  5.64 us
  transfers between devices with their start and end apart: 20, of which 9 were waited for; matrix products, arithmetic and copies ran while one was open for 0% of the time, Pallas kernels for 9%

profile of v2, /device:TPU:70, one launch (start us, length us, event | category | flops | bytes accessed | tf_op | source)
XLA Modules:
  0.0 243.0 jit_solution(8164074507784004878)
XLA Ops:
  0.7 1.1 copy-done.16
  1.7 0.7 copy-done.18
  2.4 0.7 copy-done.19
  3.1 1.5 shard_map.141
  4.6 43.8 %all-to-all-start = ((bf16[16,8,2944]{2,1,0:T(8,128)(2,1)}), bf16[16,8,2944]{2,1,0:T(8,128)(2,1)S(1)}, u32[]{:S(2)}, u32[]{:S(2)}) async-start(bf16[16,8,2944]{2,1,0:T(8,128)(2,1)} %bitcast.7), calls=%async_computation | async-start | bytes 1507328 | tf_op jit(solution)/shard_map/all_to_all | solution.py:361
  48.5 0.5 shard_map.142
  49.0 4.8 %collective-permute-start.3 = (bf16[440,1152]{1,0:T(8,128)(2,1)S(1)}, bf16[440,1152]{1,0:T(8,128)(2,1)S(1)}, u32[]{:S(2)}, u32[]{:S(2)}) collective-permute-start(bf16[440,1152]{1,0:T(8,128)(2,1)S(1)} %get-tuple-element.15.refs_0_), channel_id=1, source_target_pairs={{0,2},{2,4},{4,6},{6,8},{8,10},{10,12},{12,14},{14,0},{1,3},{3,5},... | collective-permute-start | bytes 3041288 | tf_op jit(solution)/shard_map/ppermute | solution.py:21
  53.8 2.0 collective-permute-start.5
  55.8 1.0 copy-done.14
  56.7 18.5 %collective-permute-done.3.right.refs_1_ = bf16[440,1152]{1,0:T(8,128)(2,1)S(1)} collective-permute-done((bf16[440,1152]{1,0:T(8,128)(2,1)S(1)}, bf16[440,1152]{1,0:T(8,128)(2,1)S(1)}, u32[]{:S(2)}, u32[]{:S(2)}) %collective-permute-start.3) | collective-permute-done | bytes 1013792 | tf_op jit(solution)/shard_map/ppermute | solution.py:21
  75.2 5.6 %collective-permute-start.4 = (bf16[440,1152]{1,0:T(8,128)(2,1)S(1)}, bf16[440,1152]{1,0:T(8,128)(2,1)S(1)}, u32[]{:S(2)}, u32[]{:S(2)}) collective-permute-start(bf16[440,1152]{1,0:T(8,128)(2,1)S(1)} %collective-permute-done.3.right.refs_1_), channel_id=1, source_target_pairs={{0,2},{2,4},{4,6},{6,8},{8,10},{10,12},{12,14},{14,0},{1,3},{3,5},... | collective-permute-start | bytes 3041288 | tf_op jit(solution)/shard_map/ppermute | solution.py:21
  80.9 2.0 collective-permute-start.6
  82.9 0.6 shard_map.140
  83.4 7.3 %collective-permute-start = (bf16[144,256]{1,0:T(8,128)(2,1)S(1)}, bf16[144,256]{1,0:T(8,128)(2,1)S(1)}, u32[]{:S(2)}, u32[]{:S(2)}) collective-permute-start(bf16[144,256]{1,0:T(8,128)(2,1)S(1)} %shard_map.140), channel_id=1, source_target_pairs={{0,64},{16,80},{32,96},{48,112},{64,128},{80,144},{96,160},{112,17... | collective-permute-start | bytes 221192 | tf_op jit(solution)/shard_map/ppermute | solution.py:21
  90.7 7.3 %collective-permute-start.1 = (bf16[144,256]{1,0:T(8,128)(2,1)S(1)}, bf16[144,256]{1,0:T(8,128)(2,1)S(1)}, u32[]{:S(2)}, u32[]{:S(2)}) collective-permute-start(bf16[144,256]{1,0:T(8,128)(2,1)S(1)} %shard_map.140), channel_id=1, source_target_pairs={{0,128},{16,144},{32,160},{48,176},{64,192},{80,208},{96,224},{112... | collective-permute-start | bytes 221192 | tf_op jit(solution)/shard_map/ppermute | solution.py:21
  98.1 7.3 %collective-permute-start.2 = (bf16[144,256]{1,0:T(8,128)(2,1)S(1)}, bf16[144,256]{1,0:T(8,128)(2,1)S(1)}, u32[]{:S(2)}, u32[]{:S(2)}) collective-permute-start(bf16[144,256]{1,0:T(8,128)(2,1)S(1)} %shard_map.140), channel_id=1, source_target_pairs={{0,192},{16,208},{32,224},{48,240},{64,0},{80,16},{96,32},{112,48}... | collective-permute-start | bytes 221192 | tf_op jit(solution)/shard_map/ppermute | solution.py:21
  105.4 0.8 collective-permute-done.1
  106.2 6.5 %collective-permute-done.2 = bf16[144,256]{1,0:T(8,128)(2,1)S(1)} collective-permute-done((bf16[144,256]{1,0:T(8,128)(2,1)S(1)}, bf16[144,256]{1,0:T(8,128)(2,1)S(1)}, u32[]{:S(2)}, u32[]{:S(2)}) %collective-permute-start.2) | collective-permute-done | bytes 73760 | tf_op jit(solution)/shard_map/ppermute | solution.py:21
  112.8 0.7 pad_maximum_fusion
  113.5 1.0 copy-done.3
  114.5 2.1 broadcast_in_dim.2
  116.6 3.6 %all-to-all-start.1 = ((bf16[4,576,256]{2,1,0:T(8,128)(2,1)}), bf16[4,576,256]{2,1,0:T(8,128)(2,1)S(1)}, u32[]{:S(2)}, u32[]{:S(2)}) async-start(bf16[4,576,256]{2,1,0:T(8,128)(2,1)} %broadcast_in_dim.2), calls=%async_computation.1 | async-start | bytes 2359296 | tf_op jit(solution)/shard_map/all_to_all | solution.py:30
  120.2 2.0 collective-permute-start.9
  122.2 5.2 %collective-permute-start.8 = (bf16[440,1152]{1,0:T(8,128)(2,1)}, bf16[440,1152]{1,0:T(8,128)(2,1)S(1)}, u32[]{:S(2)}, u32[]{:S(2)}) collective-permute-start(bf16[440,1152]{1,0:T(8,128)(2,1)} %copy-done.3), channel_id=1, source_target_pairs={{0,2},{2,4},{4,6},{6,8},{8,10},{10,12},{12,14},{14,0},{1,3},{3,5},... | collective-permute-start | bytes 3041288 | tf_op jit(solution)/shard_map/ppermute | solution.py:21
  127.3 2.0 collective-permute-start.7
  129.3 1.2 copy-done.1
  130.6 4.9 %collective-permute-start.14 = (bf16[288,1152]{1,0:T(8,128)(2,1)S(1)}, bf16[288,1152]{1,0:T(8,128)(2,1)S(1)}, u32[]{:S(2)}, u32[]{:S(2)}) collective-permute-start(bf16[288,1152]{1,0:T(8,128)(2,1)S(1)} %shard_map.146), channel_id=1, source_target_pairs={{0,256},{256,0},{1,257},{257,1},{2,258},{258,2},{3,259},{259,3},{4... | collective-permute-start | bytes 1990664 | tf_op jit(solution)/shard_map/ppermute | solution.py:328
  135.5 1.3 shard_map.147
  136.7 2.0 collective-permute-start.15
  138.7 9.0 %collective-permute-done.9.left.refs_1_ = bf16[440,1152]{1,0:T(8,128)(2,1)S(1)} collective-permute-done((bf16[440,1152]{1,0:T(8,128)(2,1)}, bf16[440,1152]{1,0:T(8,128)(2,1)S(1)}, u32[]{:S(2)}, u32[]{:S(2)}) %collective-permute-start.9) | collective-permute-done | bytes 1013792 | tf_op jit(solution)/shard_map/ppermute | solution.py:21
  147.7 2.0 collective-permute-start.11
  149.8 4.8 %collective-permute-start.13 = (bf16[288,1152]{1,0:T(8,128)(2,1)S(1)}, bf16[288,1152]{1,0:T(8,128)(2,1)S(1)}, u32[]{:S(2)}, u32[]{:S(2)}) collective-permute-start(bf16[288,1152]{1,0:T(8,128)(2,1)S(1)} %get-tuple-element.21), channel_id=1, source_target_pairs={{0,256},{256,0},{1,257},{257,1},{2,258},{258,2},{3,259},{259,3},{4... | collective-permute-start | bytes 1990664 | tf_op jit(solution)/shard_map/ppermute | solution.py:328
  154.6 4.9 %collective-permute-done.11.lower = bf16[144,1152]{1,0:T(8,128)(2,1)S(1)} collective-permute-done((bf16[144,1152]{1,0:T(8,128)(2,1)S(1)}, bf16[144,1152]{1,0:T(8,128)(2,1)S(1)}, u32[]{:S(2)}, u32[]{:S(2)}) %collective-permute-start.11) | collective-permute-done | bytes 331808 | tf_op jit(solution)/shard_map/ppermute | solution.py:21
  159.5 2.4 collective-permute-start.10
  162.0 5.0 %collective-permute-start.12 = (bf16[144,1152]{1,0:T(8,128)(2,1)S(1)}, bf16[144,1152]{1,0:T(8,128)(2,1)S(1)}, u32[]{:S(2)}, u32[]{:S(2)}) collective-permute-start(bf16[144,1152]{1,0:T(8,128)(2,1)S(1)} %collective-permute-done.11.lower), channel_id=1, source_target_pairs={{0,256},{256,0},{1,257},{257,1},{2,258},{258,2},{3,259},{259,3},{4... | collective-permute-start | bytes 995336 | tf_op jit(solution)/shard_map/ppermute | solution.py:328
  166.9 0.4 shard_map.144.rows
  167.3 8.1 %shard_map.148.refs_3_ = f32[640,1152]{1,0:T(8,128)S(1)} custom-call(bf16[640,1152]{1,0:T(8,128)(2,1)S(1)} %shard_map.144.rows, bf16[440,1152]{1,0:T(8,128)(2,1)S(1)} %copy-done.15, bf16[440,1152]{1,0:T(8,128)(2,1)S(1)} %collective-permute-done.3.right.refs_1_, bf16[440,1152]{1,0:T(8,128)(2,1)S(1)} %copy-done.2, bf16[440,1152]{1,0:T(8,128)(2,1)S(1)} %copy-done.4, ...), custom_call_target="tpu_custom_call" | custom-call | flops 4246732800 | bytes 11151360 | tf_op jit(solution)/shard_map/pallas_call | solution.py:50
  175.5 4.2 %collective-permute-done.13.refs_2_ = bf16[288,1152]{1,0:T(8,128)(2,1)S(1)} collective-permute-done((bf16[288,1152]{1,0:T(8,128)(2,1)S(1)}, bf16[288,1152]{1,0:T(8,128)(2,1)S(1)}, u32[]{:S(2)}, u32[]{:S(2)}) %collective-permute-start.13) | collective-permute-done | bytes 663584 | tf_op jit(solution)/shard_map/ppermute | solution.py:328
  179.7 4.0 %shard_map.149.old = f32[640,1152]{1,0:T(8,128)S(1)} custom-call(bf16[640,1152]{1,0:T(8,128)(2,1)S(1)} %shard_map.144.rows, bf16[440,1152]{1,0:T(8,128)(2,1)S(1)} %collective-permute-done.8.right.refs_0_, bf16[440,1152]{1,0:T(8,128)(2,1)S(1)} %collective-permute-done.9.left.refs_1_, ...), custom_call_target="tpu_custom_call", output_to_operand_aliasing={{}: (4, {})} | custom-call | flops 1698693120 | bytes 10063872 | tf_op jit(solution)/shard_map/pallas_call | solution.py:50
  183.7 2.9 %collective-permute-done.12.rest = bf16[144,1152]{1,0:T(8,128)(2,1)S(1)} collective-permute-done((bf16[144,1152]{1,0:T(8,128)(2,1)S(1)}, bf16[144,1152]{1,0:T(8,128)(2,1)S(1)}, u32[]{:S(2)}, u32[]{:S(2)}) %collective-permute-start.12) | collective-permute-done | bytes 331808 | tf_op jit(solution)/shard_map/ppermute | solution.py:328
  186.6 2.0 shard_map.150
  188.6 2.0 collective-permute-start.16
  190.6 2.2 collective-permute-done.16.other
  192.7 1.5 shard_map.151
  194.2 9.4 %all-to-all-start.2 = ((bf16[16,8,2944]{2,1,0:T(8,128)(2,1)}), bf16[16,8,2944]{2,1,0:T(8,128)(2,1)S(1)}, u32[]{:S(2)}, u32[]{:S(2)}) async-start(bf16[16,8,2944]{2,1,0:T(8,128)(2,1)} %bitcast.15), calls=%async_computation.2 | async-start | bytes 1507328 | tf_op jit(solution)/shard_map/all_to_all | solution.py:361
  203.7 2.7 %shard_map.143 = bf16[72,256]{1,0:T(8,128)(2,1)} custom-call(bf16[72,256]{1,0:T(8,128)(2,1)S(1)} %bitcast.28, bf16[2304,256]{1,0:T(8,128)(2,1)S(1)} %bitcast.20), custom_call_target="tpu_custom_call" | custom-call | flops 2147483648 | bytes 1253376 | tf_op jit(solution)/shard_map/pallas_call | solution.py:50
  206.4 35.2 %all-to-all-done.2 = bf16[16,8,2944]{2,1,0:T(8,128)(2,1)S(1)} async-done(((bf16[16,8,2944]{2,1,0:T(8,128)(2,1)}), bf16[16,8,2944]{2,1,0:T(8,128)(2,1)S(1)}, u32[]{:S(2)}, u32[]{:S(2)}) %all-to-all-start.2) | async-done | bytes 753696 | tf_op jit(solution)/shard_map/all_to_all | solution.py:361
  241.6 1.4 shard_map.152
  (48 shorter events, 0.3 us)
Async XLA Ops:
  0.6 47.8 %copy-start.5 = (bf16[1,1152,288]{1,2,0:T(8,128)(2,1)S(1)}, bf16[1,1152,288]{1,2,0:T(8,128)(2,1)}, u32[]{:S(2)}) copy-start(bf16[1,1152,288]{1,2,0:T(8,128)(2,1)} %param.22) | copy-start | bytes 1990660
  0.6 47.8 %copy-start.6 = (bf16[1,288,1152]{2,1,0:T(8,128)(2,1)S(1)}, bf16[1,288,1152]{2,1,0:T(8,128)(2,1)}, u32[]{:S(2)}) copy-start(bf16[1,288,1152]{2,1,0:T(8,128)(2,1)} %param.24) | copy-start | bytes 1990660
  0.7 47.8 %copy-start.12 = (f32[1,288]{1,0:T(1,128)S(1)}, f32[1,288]{1,0:T(1,128)}, u32[]{:S(2)}) copy-start(f32[1,288]{1,0:T(1,128)} %bias.2) | copy-start | bytes 3460
  0.7 1.1 copy-start.16
  1.7 0.7 copy-start.18
  2.4 0.7 copy-start.19
  4.6 78.3 %copy-start.7 = (bf16[256,72]{0,1:T(8,128)(2,1)S(1)}, bf16[256,72]{0,1:T(8,128)(2,1)}, u32[]{:S(2)}) copy-start(bf16[256,72]{0,1:T(8,128)(2,1)} %param.14) | copy-start | bytes 110596
  4.6 78.3 %copy-start.8 = (bf16[256,72]{0,1:T(8,128)(2,1)S(1)}, bf16[256,72]{0,1:T(8,128)(2,1)}, u32[]{:S(2)}) copy-start(bf16[256,72]{0,1:T(8,128)(2,1)} %param.15) | copy-start | bytes 110596
  4.6 78.3 %copy-start.9 = (bf16[256,72]{0,1:T(8,128)(2,1)S(1)}, bf16[256,72]{0,1:T(8,128)(2,1)}, u32[]{:S(2)}) copy-start(bf16[256,72]{0,1:T(8,128)(2,1)} %param.16) | copy-start | bytes 110596
  4.6 78.3 %copy-start.10 = (bf16[256,72]{0,1:T(8,128)(2,1)S(1)}, bf16[256,72]{0,1:T(8,128)(2,1)}, u32[]{:S(2)}) copy-start(bf16[256,72]{0,1:T(8,128)(2,1)} %param.17) | copy-start | bytes 110596
  4.6 78.3 %copy-start.13 = (s32[2]{0:T(128)S(1)}, s32[2]{0:T(128)}, u32[]{:S(2)}) copy-start(s32[2]{0:T(128)} %flags.1) | copy-start | bytes 28
  4.6 109.9 %all-to-all-start = ((bf16[16,8,2944]{2,1,0:T(8,128)(2,1)}), bf16[16,8,2944]{2,1,0:T(8,128)(2,1)S(1)}, u32[]{:S(2)}, u32[]{:S(2)}) async-start(bf16[16,8,2944]{2,1,0:T(8,128)(2,1)} %bitcast.7), calls=%async_computation | async-start | bytes 1507328 | tf_op jit(solution)/shard_map/all_to_all | solution.py:361
  49.0 26.2 %collective-permute-start.3 = (bf16[440,1152]{1,0:T(8,128)(2,1)S(1)}, bf16[440,1152]{1,0:T(8,128)(2,1)S(1)}, u32[]{:S(2)}, u32[]{:S(2)}) collective-permute-start(bf16[440,1152]{1,0:T(8,128)(2,1)S(1)} %get-tuple-element.15.refs_0_), channel_id=1, source_target_pairs={{0,2},{2,4},{4,6},{6,8},{8,10},{10,12},{12,14},{14,0},{1,3},{3,5},... | collective-permute-start | bytes 3041288 | tf_op jit(solution)/shard_map/ppermute | solution.py:21
  53.8 27.1 %collective-permute-start.5 = (bf16[440,1152]{1,0:T(8,128)(2,1)S(1)}, bf16[440,1152]{1,0:T(8,128)(2,1)S(1)}, u32[]{:S(2)}, u32[]{:S(2)}) collective-permute-start(bf16[440,1152]{1,0:T(8,128)(2,1)S(1)} %get-tuple-element.15.refs_0_), channel_id=1, source_target_pairs={{0,14},{2,0},{4,2},{6,4},{8,6},{10,8},{12,10},{14,12},{1,15},{3,1}... | collective-permute-start | bytes 3041288 | tf_op jit(solution)/shard_map/ppermute | solution.py:21
  55.7 1.0 copy-start.14
  75.2 38.3 %collective-permute-start.4 = (bf16[440,1152]{1,0:T(8,128)(2,1)S(1)}, bf16[440,1152]{1,0:T(8,128)(2,1)S(1)}, u32[]{:S(2)}, u32[]{:S(2)}) collective-permute-start(bf16[440,1152]{1,0:T(8,128)(2,1)S(1)} %collective-permute-done.3.right.refs_1_), channel_id=1, source_target_pairs={{0,2},{2,4},{4,6},{6,8},{8,10},{10,12},{12,14},{14,0},{1,3},{3,5},... | collective-permute-start | bytes 3041288 | tf_op jit(solution)/shard_map/ppermute | solution.py:21
  80.9 35.7 %copy-start = (bf16[440,1152]{1,0:T(8,128)(2,1)}, bf16[440,1152]{1,0:T(8,128)(2,1)S(1)}, u32[]{:S(2)}) copy-start(bf16[440,1152]{1,0:T(8,128)(2,1)S(1)} %collective-permute-done.5.left.refs_2_) | copy-start | bytes 3041284
  80.9 33.6 %collective-permute-start.6 = (bf16[440,1152]{1,0:T(8,128)(2,1)S(1)}, bf16[440,1152]{1,0:T(8,128)(2,1)}, u32[]{:S(2)}, u32[]{:S(2)}) collective-permute-start(bf16[440,1152]{1,0:T(8,128)(2,1)S(1)} %collective-permute-done.5.left.refs_2_), channel_id=1, source_target_pairs={{0,14},{2,0},{4,2},{6,4},{8,6},{10,8},{12,10},{14,12},{1,15},{3,1}... | collective-permute-start | bytes 3041288 | tf_op jit(solution)/shard_map/ppermute | solution.py:21
  83.4 21.9 %collective-permute-start = (bf16[144,256]{1,0:T(8,128)(2,1)S(1)}, bf16[144,256]{1,0:T(8,128)(2,1)S(1)}, u32[]{:S(2)}, u32[]{:S(2)}) collective-permute-start(bf16[144,256]{1,0:T(8,128)(2,1)S(1)} %shard_map.140), channel_id=1, source_target_pairs={{0,64},{16,80},{32,96},{48,112},{64,128},{80,144},{96,160},{112,17... | collective-permute-start | bytes 221192 | tf_op jit(solution)/shard_map/ppermute | solution.py:21
  90.7 15.5 %collective-permute-start.1 = (bf16[144,256]{1,0:T(8,128)(2,1)S(1)}, bf16[144,256]{1,0:T(8,128)(2,1)S(1)}, u32[]{:S(2)}, u32[]{:S(2)}) collective-permute-start(bf16[144,256]{1,0:T(8,128)(2,1)S(1)} %shard_map.140), channel_id=1, source_target_pairs={{0,128},{16,144},{32,160},{48,176},{64,192},{80,208},{96,224},{112... | collective-permute-start | bytes 221192 | tf_op jit(solution)/shard_map/ppermute | solution.py:21
  98.1 14.7 %collective-permute-start.2 = (bf16[144,256]{1,0:T(8,128)(2,1)S(1)}, bf16[144,256]{1,0:T(8,128)(2,1)S(1)}, u32[]{:S(2)}, u32[]{:S(2)}) collective-permute-start(bf16[144,256]{1,0:T(8,128)(2,1)S(1)} %shard_map.140), channel_id=1, source_target_pairs={{0,192},{16,208},{32,224},{48,240},{64,0},{80,16},{96,32},{112,48}... | collective-permute-start | bytes 221192 | tf_op jit(solution)/shard_map/ppermute | solution.py:21
  113.5 1.0 copy-start.3
  116.6 77.7 %all-to-all-start.1 = ((bf16[4,576,256]{2,1,0:T(8,128)(2,1)}), bf16[4,576,256]{2,1,0:T(8,128)(2,1)S(1)}, u32[]{:S(2)}, u32[]{:S(2)}) async-start(bf16[4,576,256]{2,1,0:T(8,128)(2,1)} %broadcast_in_dim.2), calls=%async_computation.1 | async-start | bytes 2359296 | tf_op jit(solution)/shard_map/all_to_all | solution.py:30
  120.2 27.5 %collective-permute-start.9 = (bf16[440,1152]{1,0:T(8,128)(2,1)}, bf16[440,1152]{1,0:T(8,128)(2,1)S(1)}, u32[]{:S(2)}, u32[]{:S(2)}) collective-permute-start(bf16[440,1152]{1,0:T(8,128)(2,1)} %collective-permute-done.6.left.refs_4_), channel_id=1, source_target_pairs={{0,14},{2,0},{4,2},{6,4},{8,6},{10,8},{12,10},{14,12},{1,15},{3,1}... | collective-permute-start | bytes 3041288 | tf_op jit(solution)/shard_map/ppermute | solution.py:21
  122.2 27.5 %collective-permute-start.8 = (bf16[440,1152]{1,0:T(8,128)(2,1)}, bf16[440,1152]{1,0:T(8,128)(2,1)S(1)}, u32[]{:S(2)}, u32[]{:S(2)}) collective-permute-start(bf16[440,1152]{1,0:T(8,128)(2,1)} %copy-done.3), channel_id=1, source_target_pairs={{0,2},{2,4},{4,6},{6,8},{8,10},{10,12},{12,14},{14,0},{1,3},{3,5},... | collective-permute-start | bytes 3041288 | tf_op jit(solution)/shard_map/ppermute | solution.py:21
  127.3 34.6 %collective-permute-start.7 = (bf16[128,2944]{1,0:T(8,128)(2,1)S(1)}, bf16[128,2944]{1,0:T(8,128)(2,1)S(1)}, u32[]{:S(2)}, u32[]{:S(2)}) collective-permute-start(bf16[128,2944]{1,0:T(8,128)(2,1)S(1)} %bitcast.18), channel_id=1, source_target_pairs={{0,1},{1,0},{2,3},{3,2},{4,5},{5,4},{6,7},{7,6},{8,9},{9,8},{10,11... | collective-permute-start | bytes 2261000 | tf_op jit(solution)/shard_map/ppermute | solution.py:21
  129.3 1.2 copy-start.1
  130.5 5.0 %copy-start.4 = (bf16[440,1152]{1,0:T(8,128)(2,1)S(1)}, bf16[440,1152]{1,0:T(8,128)(2,1)}, u32[]{:S(2)}) copy-start(bf16[440,1152]{1,0:T(8,128)(2,1)} %copy-done.3) | copy-start | bytes 3041284
  130.6 36.8 %collective-permute-start.14 = (bf16[288,1152]{1,0:T(8,128)(2,1)S(1)}, bf16[288,1152]{1,0:T(8,128)(2,1)S(1)}, u32[]{:S(2)}, u32[]{:S(2)}) collective-permute-start(bf16[288,1152]{1,0:T(8,128)(2,1)S(1)} %shard_map.146), channel_id=1, source_target_pairs={{0,256},{256,0},{1,257},{257,1},{2,258},{258,2},{3,259},{259,3},{4... | collective-permute-start | bytes 1990664 | tf_op jit(solution)/shard_map/ppermute | solution.py:328
  136.7 30.6 %collective-permute-start.15 = (bf16[288,1152]{1,0:T(8,128)(2,1)S(1)}, bf16[288,1152]{1,0:T(8,128)(2,1)S(1)}, u32[]{:S(2)}, u32[]{:S(2)}) collective-permute-start(bf16[288,1152]{1,0:T(8,128)(2,1)S(1)} %shard_map.147), channel_id=1, source_target_pairs={{0,256},{256,0},{1,257},{257,1},{2,258},{258,2},{3,259},{259,3},{4... | collective-permute-start | bytes 1990664 | tf_op jit(solution)/shard_map/ppermute | solution.py:328
  147.7 11.8 %collective-permute-start.11 = (bf16[144,1152]{1,0:T(8,128)(2,1)S(1)}, bf16[144,1152]{1,0:T(8,128)(2,1)S(1)}, u32[]{:S(2)}, u32[]{:S(2)}) collective-permute-start(bf16[144,1152]{1,0:T(8,128)(2,1)S(1)} %slice.4), channel_id=1, source_target_pairs={{0,14},{2,0},{4,2},{6,4},{8,6},{10,8},{12,10},{14,12},{1,15},{3,1}... | collective-permute-start | bytes 995336 | tf_op jit(solution)/shard_map/ppermute | solution.py:21
  149.8 29.9 %collective-permute-start.13 = (bf16[288,1152]{1,0:T(8,128)(2,1)S(1)}, bf16[288,1152]{1,0:T(8,128)(2,1)S(1)}, u32[]{:S(2)}, u32[]{:S(2)}) collective-permute-start(bf16[288,1152]{1,0:T(8,128)(2,1)S(1)} %get-tuple-element.21), channel_id=1, source_target_pairs={{0,256},{256,0},{1,257},{257,1},{2,258},{258,2},{3,259},{259,3},{4... | collective-permute-start | bytes 1990664 | tf_op jit(solution)/shard_map/ppermute | solution.py:328
  159.5 7.8 %copy-start.2 = (bf16[440,1152]{1,0:T(8,128)(2,1)S(1)}, bf16[440,1152]{1,0:T(8,128)(2,1)}, u32[]{:S(2)}) copy-start(bf16[440,1152]{1,0:T(8,128)(2,1)} %copy-done) | copy-start | bytes 3041284
  159.5 7.8 %copy-start.15 = (bf16[440,1152]{1,0:T(8,128)(2,1)S(1)}, bf16[440,1152]{1,0:T(8,128)(2,1)}, u32[]{:S(2)}) copy-start(bf16[440,1152]{1,0:T(8,128)(2,1)} %copy-done.14) | copy-start | bytes 3041284
  159.5 27.1 %collective-permute-start.10 = (bf16[296,1152]{1,0:T(8,128)(2,1)S(1)}, bf16[296,1152]{1,0:T(8,128)(2,1)S(1)}, u32[]{:S(2)}, u32[]{:S(2)}) collective-permute-start(bf16[296,1152]{1,0:T(8,128)(2,1)S(1)} %get-tuple-element.20), channel_id=1, source_target_pairs={{0,2},{2,4},{4,6},{6,8},{8,10},{10,12},{12,14},{14,0},{1,3},{3,5},... | collective-permute-start | bytes 2045960 | tf_op jit(solution)/shard_map/ppermute | solution.py:21
  162.0 24.6 %collective-permute-start.12 = (bf16[144,1152]{1,0:T(8,128)(2,1)S(1)}, bf16[144,1152]{1,0:T(8,128)(2,1)S(1)}, u32[]{:S(2)}, u32[]{:S(2)}) collective-permute-start(bf16[144,1152]{1,0:T(8,128)(2,1)S(1)} %collective-permute-done.11.lower), channel_id=1, source_target_pairs={{0,256},{256,0},{1,257},{257,1},{2,258},{258,2},{3,259},{259,3},{4... | collective-permute-start | bytes 995336 | tf_op jit(solution)/shard_map/ppermute | solution.py:328
  183.7 9.0 %copy-start.11 = (f32[1,1152]{1,0:T(1,128)S(1)}, f32[1,1152]{1,0:T(1,128)}, u32[]{:S(2)}) copy-start(f32[1,1152]{1,0:T(1,128)} %bias.3) | copy-start | bytes 13828
  188.6 4.1 %collective-permute-start.16 = (bf16[320,1152]{1,0:T(8,128)(2,1)S(1)}, bf16[320,1152]{1,0:T(8,128)(2,1)S(1)}, u32[]{:S(2)}, u32[]{:S(2)}) collective-permute-start(bf16[320,1152]{1,0:T(8,128)(2,1)S(1)} %get-tuple-element.24), channel_id=1, source_target_pairs={{0,1},{1,0},{2,3},{3,2},{4,5},{5,4},{6,7},{7,6},{8,9},{9,8},{10,11... | collective-permute-start | bytes 2211848 | tf_op jit(solution)/shard_map/ppermute | solution.py:21
  194.2 9.4 %copy-start.17 = (bf16[256,72]{0,1:T(8,128)(2,1)S(1)}, bf16[256,72]{0,1:T(8,128)(2,1)}, u32[]{:S(2)}) copy-start(bf16[256,72]{0,1:T(8,128)(2,1)} %param.13) | copy-start | bytes 110596
  194.2 47.4 %all-to-all-start.2 = ((bf16[16,8,2944]{2,1,0:T(8,128)(2,1)}), bf16[16,8,2944]{2,1,0:T(8,128)(2,1)S(1)}, u32[]{:S(2)}, u32[]{:S(2)}) async-start(bf16[16,8,2944]{2,1,0:T(8,128)(2,1)} %bitcast.15), calls=%async_computation.2 | async-start | bytes 1507328 | tf_op jit(solution)/shard_map/all_to_all | solution.py:361
